TPU v7x, 16 devices: a 4x2x1 block of a 4x4x8 slice. The times are simulated.
16 devices in a mesh: dp: 2 (over y, z), tp: 8 (over x, core).
Axes of the slice: x: 4, y: 2, z: 1, core: 2. Of those that a mesh axis runs over, the one named last changes fastest.
The devices are a block of a 4x4x8 slice.
Arguments:
- x_in: bfloat16 [16, 1536, 2048], P('dp', 'tp'), parts along dimension 0
- ln_scale: bfloat16 [2048], replicated
- w_q: bfloat16 [2048, 2048], P(None, 'tp')
- w_k: bfloat16 [2048, 256], replicated
- w_v: bfloat16 [2048, 256], replicated
- w_o: bfloat16 [2048, 2048], P('tp')
- grad_y: bfloat16 [16, 1536, 2048], P('dp', 'tp'), parts along dimension 0
Outputs:
- output 1: bfloat16 [16, 1536, 2048], P('dp', 'tp'), parts along dimension 0
- output 2: bfloat16 [16, 1536, 2048], P('dp', 'tp'), parts along dimension 0
- output 3: float32 [4096], P('dp'), parts along dimension 0
- output 4: bfloat16 [4096, 2048], P('dp', 'tp'), parts along dimension 0
- output 5: float32 [4096, 256], P('dp'), parts along dimension 0
- output 6: float32 [4096, 256], P('dp'), parts along dimension 0
- output 7: bfloat16 [4096, 2048], P(('dp', 'tp')), parts along dimension 0
There are 2 independent parts. A program takes and returns all parts, laid end to end along the dimension named above; an argument that names none is the same for every part.
All inputs are finite; a program needn't handle non-finite values.
Results may differ from a plain program's by a relative error of at most 0.0158944.
Values are sent between devices in bfloat16 or wider.
A program may use at most 768 MiB of HBM per device.

v0:
```python
import functools
import jax
import jax.numpy as jnp
from jax import lax
from jax.experimental import pallas as pl
from jax.experimental.pallas import tpu as pltpu
from jax.sharding import PartitionSpec as P

LN_EPS = 1e-6
ROPE_BASE = 10000.0
LOG2E = 1.4426950408889634
F32 = jnp.float32
BF16 = jnp.bfloat16


def rope_tables(positions, head_dim):
    half_dim = head_dim // 2
    inv_freq = ROPE_BASE ** (-2.0 * jnp.arange(half_dim, dtype=F32) / head_dim)
    angles = positions.astype(F32)[:, None] * inv_freq[None, :]
    return jnp.cos(angles), jnp.sin(angles)


def rotate(vectors, cos_t, sin_t):
    half_dim = vectors.shape[-1] // 2
    lo_half = vectors[..., :half_dim]
    hi_half = vectors[..., half_dim:]
    return jnp.concatenate([lo_half * cos_t - hi_half * sin_t, hi_half * cos_t + lo_half * sin_t], axis=-1)


def dot_nn(a, b):
    return lax.dot_general(a, b, (((1,), (0,)), ((), ())), preferred_element_type=F32)


def dot_nt(a, b):
    return lax.dot_general(a, b, (((1,), (1,)), ((), ())), preferred_element_type=F32)


def attn_body(n_heads, tok, seq, d, group, q_ref, do_ref, kv_ref, cos_ref, sin_ref,
              o_ref, dq_ref, dkv_ref, bias, s_buf, p_buf, ds_buf):
    scale = d ** -0.5
    rows = group * tok
    kb = 256
    half = d // 2

    @pl.when(pl.program_id(0) == 0)
    def _():
        t0 = lax.axis_index('tp') * tok
        row = lax.broadcasted_iota(jnp.int32, (tok, seq), 0) + t0
        col = lax.broadcasted_iota(jnp.int32, (tok, seq), 1)
        bias[...] = jnp.where(col <= row, F32(3.0e38), F32(-1e30))

    for g in range(n_heads // group):
        q = jnp.concatenate([q_ref[0, g * group + j] for j in range(group)], axis=0)
        do = jnp.concatenate([do_ref[0, g * group + j] for j in range(group)], axis=0)
        for c in range(seq // kb):
            cols = slice(c * kb, (c + 1) * kb)
            s_buf[:, cols] = dot_nt(q, kv_ref[0, cols, :d])
        rb = 16
        for r in range(rows // rb):
            rs = slice(r * rb, (r + 1) * rb)
            t = (r * rb) % tok
            s = jnp.minimum(s_buf[rs, :], bias[t:t + rb, :])
            m = jnp.max(s, axis=1, keepdims=True)
            e = jnp.exp2(s * (scale * LOG2E) - m * (scale * LOG2E))
            l = jnp.sum(e, axis=1, keepdims=True)
            p_buf[rs, :] = (e * (1.0 / l)).astype(BF16)
        o = dot_nn(p_buf[...], kv_ref[0, :, d:])
        dvec = jnp.sum(o * do.astype(F32), axis=1, keepdims=True)
        o16 = o.astype(BF16)
        for j in range(group):
            o_ref[0, g * group + j] = o16[j * tok:(j + 1) * tok]
        dv_t = dot_nn(do.T, p_buf[...])
        for c in range(seq // kb):
            cols = slice(c * kb, (c + 1) * kb)
            dp = dot_nt(do, kv_ref[0, cols, d:])
            ds_buf[:, cols] = (p_buf[:, cols].astype(F32) * (dp - dvec)).astype(BF16)
        dq = dot_nn(ds_buf[...], kv_ref[0, :, :d]) * scale
        dk_t = dot_nn(q.T, ds_buf[...])
        for j in range(group):
            part = dq[j * tok:(j + 1) * tok]
            lo, hi = part[:, :half], part[:, half:]
            cs, sn = cos_ref[...], sin_ref[...]
            dq_ref[0, g * group + j, :, :half] = (lo * cs + hi * sn).astype(BF16)
            dq_ref[0, g * group + j, :, half:] = (hi * cs - lo * sn).astype(BF16)
        if g == 0:
            dk_acc, dv_acc = dk_t, dv_t
        else:
            dk_acc = dk_acc + dk_t
            dv_acc = dv_acc + dv_t
    dkv_ref[0, :, :d] = (dk_acc * scale).T.astype(BF16)
    dkv_ref[0, :, d:] = dv_acc.T.astype(BF16)


def attention(q, do, kv, cos_t, sin_t):
    n_batch, n_heads, tok, d = q.shape
    seq = kv.shape[1]
    group = 4
    rows = group * tok
    head_spec = pl.BlockSpec((1, n_heads, tok, d), lambda b: (b, 0, 0, 0))
    kv_spec = pl.BlockSpec((1, seq, 2 * d), lambda b: (b, 0, 0))
    tab_spec = pl.BlockSpec((tok, d // 2), lambda b: (0, 0))
    return pl.pallas_call(
        functools.partial(attn_body, n_heads, tok, seq, d, group),
        grid=(n_batch,),
        in_specs=[head_spec, head_spec, kv_spec, tab_spec, tab_spec],
        out_specs=[head_spec, head_spec, kv_spec],
        out_shape=[jax.ShapeDtypeStruct(q.shape, BF16), jax.ShapeDtypeStruct(q.shape, BF16),
                   jax.ShapeDtypeStruct(kv.shape, BF16)],
        scratch_shapes=[pltpu.VMEM((tok, seq), F32), pltpu.VMEM((rows, seq), F32),
                        pltpu.VMEM((rows, seq), BF16), pltpu.VMEM((rows, seq), BF16)],
        compiler_params=pltpu.CompilerParams(dimension_semantics=("arbitrary",), vmem_limit_bytes=56 * 2**20),
        cost_estimate=pl.CostEstimate(flops=12 * n_batch * n_heads * tok * seq * d, bytes_accessed=40 * 2**20,
                                      transcendentals=n_batch * n_heads * tok * seq),
        name="attention",
    )(q, do, kv, cos_t, sin_t)


def rdma(src, dst, send, recv, to):
    return pltpu.make_async_remote_copy(src_ref=src, dst_ref=dst, send_sem=send, recv_sem=recv,
                                        device_id={'tp': to}, device_id_type=pl.DeviceIdType.MESH)


def ring_ids():
    me = lax.axis_index('tp')
    k = lax.rem(me, 2)
    return me, k, me + 1 - 2 * k, lax.rem(me + 2, 8), lax.rem(me + 6, 8)


def enter(peers):
    barrier = pltpu.get_barrier_semaphore()
    for p in peers:
        pl.semaphore_signal(barrier, inc=1, device_id={'tp': p}, device_id_type=pl.DeviceIdType.MESH)
    pl.semaphore_wait(barrier, len(peers))


def proj_body(nb, tok, x_hbm, g_ref, wq_hbm, wkv_ref, wo_hbm, dy_hbm, cos_ref, sin_ref,
              hn_hbm, q_hbm, do_hbm, kv_hbm, wqf_hbm, wof_hbm,
              x_v, hn_v, dy_v, wq_v, wo_v, kv_v, out_v,
              send, recv, x_sem, dy_sem, own_sem, out_sem, misc_sem, w_sem):
    n_tok, e = x_hbm.shape
    d = kv_v.shape[1] // 2
    half = d // 2
    mc = 2 * tok
    me, k, mate, cw, ccw = ring_ids()
    base = 2 * (me // 2)

    def head(off, par):
        return lax.rem(base + 2 * off + 8, 8) + par
    enter((mate, cw, ccw))

    fulls = (wq_v, wo_v)
    locs = (wq_hbm, wo_hbm)

    def half_of(w, ref, j):
        n = ref.shape[0] // 2
        return ref.at[pl.ds(j * n, n)]

    sends = []

    def send_full(w, h, j, to, own=False):
        src = locs[w] if own else fulls[w].at[h]
        c = rdma(src, fulls[w].at[h], send.at[w, j], recv.at[w, j], to)
        c.start()
        sends.append(c)

    def send_half(w, h, part, j, to):
        c = rdma(half_of(w, fulls[w].at[h], part), half_of(w, fulls[w].at[h], part), send.at[w, j], recv.at[w, j], to)
        c.start()
        sends.append(c)

    def wait_full(w, h, j):
        rdma(fulls[w].at[h], fulls[w].at[h], send.at[w, j], recv.at[w, j], mate).wait_recv()

    def wait_half(w, h, part, j):
        ref = half_of(w, fulls[w].at[h], part)
        rdma(ref, ref, send.at[w, j], recv.at[w, j], mate).wait_recv()

    for w in range(2):
        send_full(w, me, 0, cw, True)
        send_full(w, me, 1, ccw, True)
        send_full(w, me, 4, mate, True)
    own = [pltpu.make_async_copy(locs[w], fulls[w].at[me], own_sem.at[w]) for w in range(2)]
    xs = [pltpu.make_async_copy(x_hbm.at[pl.ds(b * tok, tok)], x_v.at[pl.ds(b * tok, tok)], x_sem.at[b]) for b in range(nb)]
    for c in xs:
        c.start()
    for c in own:
        c.start()
    dyc = pltpu.make_async_copy(dy_hbm, dy_v, dy_sem)
    dyc.start()

    gain = g_ref[...].astype(F32)
    for b in range(nb):
        xs[b].wait()

        @pl.loop(0, tok // 16, unroll=2)
        def _(r):
            rs = pl.ds(pl.multiple_of(b * tok + r * 16, 16), 16)
            x = x_v[rs, :].astype(F32)
            c = x - jnp.mean(x, axis=1, keepdims=True)
            inv = lax.rsqrt(jnp.mean(c * c, axis=1, keepdims=True) + LN_EPS)
            hn_v[rs, :] = (c * inv * gain).astype(BF16)
    hn_out = pltpu.make_async_copy(hn_v, hn_hbm, misc_sem.at[0])
    hn_out.start()

    def rope_rows(raw):
        lo, hi = raw[:, :half], raw[:, half:d]
        cs, sn = cos_ref[...], sin_ref[...]
        return lo * cs - hi * sn, hi * cs + lo * sn

    @pl.loop(0, n_tok // mc)
    def _(i):
        rs = pl.ds(pl.multiple_of(i * mc, mc), mc)
        raw = dot_nn(hn_v[rs, :], wkv_ref[...])
        lo, hi = rope_rows(raw)
        kv_v[rs, :half] = lo.astype(BF16)
        kv_v[rs, half:d] = hi.astype(BF16)
        kv_v[rs, d:] = raw[:, d:].astype(BF16)
    kv_out = pltpu.make_async_copy(kv_v, kv_hbm, misc_sem.at[1])
    kv_out.start()

    outs = []
    saves = []

    def save(w, h):
        c = pltpu.make_async_copy(fulls[w].at[h], (wqf_hbm, wof_hbm)[w].at[h], w_sem.at[len(saves)])
        c.start()
        saves.append(c)

    def project(w, h):
        slot = len(outs) % 4
        if len(outs) >= 4:
            outs[-4].wait()

        @pl.loop(0, n_tok // mc)
        def _(i):
            rs = pl.ds(pl.multiple_of(i * mc, mc), mc)
            if w == 0:
                lo, hi = rope_rows(dot_nn(hn_v[rs, :], wq_v[h]))
                o0 = lo.reshape(2, tok, half).astype(BF16)
                o1 = hi.reshape(2, tok, half).astype(BF16)
                out_v[slot, pl.ds(2 * i, 2), :, :half] = o0
                out_v[slot, pl.ds(2 * i, 2), :, half:] = o1
            else:
                out_v[slot, pl.ds(2 * i, 2)] = dot_nt(dy_v[rs, :], wo_v[h]).reshape(2, tok, d).astype(BF16)
        c = pltpu.make_async_copy(out_v.at[slot], (q_hbm, do_hbm)[w].at[:, h], out_sem.at[slot])
        c.start()
        outs.append(c)
        save(w, h)

    other = 1 - k
    for w in range(2):
        own[w].wait()
        if w == 1:
            dyc.wait()
        project(w, me)
        wait_full(w, mate, 4)
        project(w, mate)
    for w in range(2):
        wait_full(w, head(-1, k), 0)
        send_half(w, head(-1, k), 0, 2, cw)
        wait_full(w, head(1, k), 1)
        send_half(w, head(1, k), 1, 3, ccw)
        send_full(w, head(-1, k), 5, mate)
        send_full(w, head(1, k), 6, mate)
        project(w, head(-1, k))
        project(w, head(1, k))
        wait_full(w, head(-1, other), 5)
        project(w, head(-1, other))
        wait_full(w, head(1, other), 6)
        project(w, head(1, other))
    for w in range(2):
        wait_half(w, head(2, k), 0, 2)
        send_half(w, head(2, k), 0, 7, mate)
        wait_half(w, head(2, k), 1, 3)
        send_half(w, head(2, k), 1, 8, mate)
        project(w, head(2, k))
        wait_half(w, head(2, other), 0, 7)
        wait_half(w, head(2, other), 1, 8)
        project(w, head(2, other))
    for c in outs[-4:] + saves + [hn_out, kv_out]:
        c.wait()
    for c in sends:
        c.wait_send()


def project(x, gain, wq, w_kv, wo, dy, cos_t, sin_t):
    nb, tok, e = x.shape
    d = wq.shape[1]
    n_heads = 8
    n_tok = nb * tok
    any_spec = pl.BlockSpec(memory_space=pl.ANY)
    vmem = pl.BlockSpec(memory_space=pltpu.VMEM)
    act = jax.ShapeDtypeStruct((nb, n_heads, tok, d), BF16)
    dma = pltpu.SemaphoreType.DMA
    flops = 2 * n_tok * e * (2 * n_heads + 2) * d
    cos2, sin2 = jnp.tile(cos_t, (2, 1)), jnp.tile(sin_t, (2, 1))
    hn, q, do, kv, wqf, wof = pl.pallas_call(
        functools.partial(proj_body, nb, tok),
        in_specs=[any_spec, vmem, any_spec, vmem, any_spec, any_spec, vmem, vmem],
        out_specs=[any_spec] * 6,
        out_shape=[jax.ShapeDtypeStruct((n_tok, e), BF16), act, act, jax.ShapeDtypeStruct((n_tok, 2 * d), BF16),
                   jax.ShapeDtypeStruct((n_heads, e, d), BF16), jax.ShapeDtypeStruct((n_heads, d, e), BF16)],
        scratch_shapes=[pltpu.VMEM((n_tok, e), BF16), pltpu.VMEM((n_tok, e), BF16), pltpu.VMEM((n_tok, e), BF16),
                        pltpu.VMEM((n_heads, e, d), BF16), pltpu.VMEM((n_heads, d, e), BF16),
                        pltpu.VMEM((n_tok, 2 * d), BF16), pltpu.VMEM((4, nb, tok, d), BF16),
                        dma((2, 9)), dma((2, 9)), dma((nb,)), dma(()), dma((2,)), dma((4,)), dma((2,)), dma((16,))],
        compiler_params=pltpu.CompilerParams(collective_id=0, has_side_effects=True, vmem_limit_bytes=60 * 2**20),
        cost_estimate=pl.CostEstimate(flops=flops, bytes_accessed=60 * 2**20, transcendentals=0),
        name="project",
    )(x.reshape(n_tok, e), gain.reshape(1, e), wq, w_kv, wo, dy.reshape(n_tok, e), cos2, sin2)
    return hn.reshape(nb, tok, e), q, do, kv.reshape(nb, tok, 2 * d), wqf, wof


def solution(mesh):
    act_spec = P('dp', 'tp', None)

    def device_step(x_loc, ln_scale, wq_loc, w_k, w_v, wo_loc, dy_loc):
        n_batch, tok, model_dim = x_loc.shape
        d = w_k.shape[1]
        t0 = lax.axis_index('tp') * tok
        cos_t, sin_t = rope_tables(t0 + jnp.arange(tok), d)

        w_kv = jnp.concatenate([w_k, w_v], axis=1)
        hn, q, do, kv_loc, wq_h, wo_h = project(x_loc, ln_scale, wq_loc, w_kv, wo_loc, dy_loc, cos_t, sin_t)
        kv_full = lax.all_gather(kv_loc, 'tp', axis=1, tiled=True)
        x_f32 = x_loc.astype(F32)
        centered = x_f32 - jnp.mean(x_f32, axis=-1, keepdims=True)
        inv_std = lax.rsqrt(jnp.mean(centered * centered, axis=-1, keepdims=True) + LN_EPS)
        x_hat = centered * inv_std
        ln_gain = ln_scale.astype(F32)

        o, dq, dkv = attention(q, do, kv_full, cos_t, sin_t)

        dkv_loc = lax.psum_scatter(dkv, 'tp', scatter_dimension=1, tiled=True)
        gwo = jnp.einsum('bhtd,bte->hde', o, dy_loc, preferred_element_type=F32)
        gwo = lax.psum_scatter(gwo, 'tp', scatter_dimension=0, tiled=True)[0].astype(BF16)
        gwq = jnp.einsum('bte,bhtd->hed', hn, dq, preferred_element_type=F32)
        gwq = lax.psum_scatter(gwq, 'tp', scatter_dimension=0, tiled=True)[0].astype(BF16)
        y = (x_f32 + jnp.einsum('bhtd,hde->bte', o, wo_h, preferred_element_type=F32)).astype(BF16)

        dk_loc = rotate(dkv_loc[..., :d].astype(F32), cos_t, -sin_t).astype(BF16)
        dkv_loc = jnp.concatenate([dk_loc, dkv_loc[..., d:]], axis=-1)
        gwkv = jnp.einsum('bte,btd->ed', hn, dkv_loc, preferred_element_type=F32)
        gwkv = lax.psum(gwkv, 'tp')
        dhn = jnp.einsum('bhtd,hed->bte', dq, wq_h, preferred_element_type=F32)
        dhn = dhn + jnp.einsum('btd,ed->bte', dkv_loc, w_kv, preferred_element_type=F32)
        d_hat = dhn * ln_gain
        grad_ln = lax.psum(jnp.sum(dhn * x_hat, axis=(0, 1)), 'tp')
        grad_x = inv_std * (d_hat - jnp.mean(d_hat, axis=-1, keepdims=True) - x_hat * jnp.mean(d_hat * x_hat, axis=-1, keepdims=True)) + dy_loc.astype(F32)
        return y, grad_x.astype(BF16), grad_ln, gwq, gwkv[:, :d], gwkv[:, d:], gwo

    return jax.shard_map(device_step, mesh=mesh, in_specs=(act_spec, P(None), P(None, 'tp'), P(None, None), P(None, None), P('tp', None), act_spec), out_specs=(act_spec, act_spec, P('dp'), P('dp', 'tp'), P('dp', None), P('dp', None), P(('dp', 'tp'), None)), check_vma=False)
```

profile of v0, /device:TPU:112, one launch (start us, length us, event | category | flops | bytes accessed | tf_op | source)
XLA Modules:
  0.0 587.3 jit_solution(16238633149617999669)
XLA Ops:
  7.3 1.3 constant_dynamic-update-slice_fusion.1
  8.6 1.3 reshape.178.g_ref
  9.9 0.4 fusion.24
  10.3 1.4 constant_dynamic-update-slice_fusion.wkv_ref
  11.7 0.8 tile.8
  12.5 0.7 tile.20
  13.2 80.9 %project.1 = (bf16[1536,2048]{1,0:T(8,128)(2,1)}, bf16[8,8,192,256]{3,2,1,0:T(8,128)(2,1)}, bf16[8,8,192,256]{3,2,1,0:T(8,128)(2,1)}, bf16[1536,512]{1,0:T(8,128...) custom-call(bf16[1536,2048]{1,0:T(8,128)(2,1)} %bitcast.54, bf16[1,2048]{1,0:T(2,128)(2,1)} %reshape.178.g_ref, ...), custom_call_target="tpu_custom_call" | custom-call | flops 28991029248 | bytes 62914560 | tf_op jit(solution)/shard_map/project/pallas_call | solution.py:297
  94.2 0.2 reduce-scatter.4.cloned.1.call-start
  94.5 64.3 %all-gather.2.cloned.1.call-done.kv_ref = bf16[8,1536,512]{2,1,0:T(8,128)(2,1)} async-done(((bf16[8,192,512]{2,1,0:T(8,128)(2,1)}), bf16[8,1536,512]{2,1,0:T(8,128)(2,1)}) %all-gather.2.cloned.1.call-update) | async-done | bytes 12582928 | tf_op jit(solution)/shard_map/all_gather | solution.py:325
  158.8 96.2 %attention.1 = (bf16[8,8,192,256]{3,2,1,0:T(8,128)(2,1)}, bf16[8,8,192,256]{3,2,1,0:T(8,128)(2,1)}, bf16[8,1536,512]{2,1,0:T(8,128)(2,1)}) custom-call(bf16[8,8,192,256]{3,2,1,0:T(8,128)(2,1)} %get-tuple-element.16.q_ref, bf16[8,8,192,256]{3,2,1,0:T(8,128)(2,1)} %get-tuple-element.17.do_ref, bf16[8,1536,512]{2,1,0:T(8,128)(2,1)} %all-gather.2.cloned.1.call-done.kv_ref, ...), custom_call_target="tpu_custom_call" | custom-call | flops 57982058496 | bytes 41943040 | tf_op jit(solution)/shard_map/attention/pallas_call | solution.py:102
  255.1 0.3 all-reduce.2.cloned.1.call-start
  255.4 68.5 %reduce-scatter.4.cloned.1.call-done = bf16[8,192,512]{2,1,0:T(8,128)(2,1)} async-done(((bf16[8,1536,512]{2,1,0:T(8,128)(2,1)}), bf16[8,192,512]{2,1,0:T(8,128)(2,1)}) %reduce-scatter.4.cloned.1.call-update) | async-done | bytes 1572880 | tf_op jit(solution)/shard_map/reduce_scatter | solution.py:334
  324.0 1.6 slice_convert_fusion
  325.6 0.2 subtract_convert_fusion
  325.8 8.3 %convolution_bitcast_fusion.2 = f32[2048,512]{1,0:T(8,128)} fusion(bf16[8,192,2048]{2,1,0:T(8,128)(2,1)} %bitcast.59, bf16[8,192,256]{2,1,0:T(8,128)(2,1)S(1)} %get-tuple-element.40, bf16[8,192,128]{2,1,0:T(8,128)(2,1)S(1)} %get-tuple-element.38, bf16[8,192,128]{2,1,0:T(8,128)(2,1)S(1)} %get-tuple-element.37), kind=kOutput, calls=%fused_computation.25 | convolution fusion | flops 3225944064 | bytes 12058624 | tf_op jit(solution)/shard_map/bte,btd->ed/dot_general | solution.py:343
  334.2 20.7 %convolution_bitcast_fusion.1 = f32[8,2048,256]{1,2,0:T(8,128)} fusion(bf16[8,8,192,256]{3,2,1,0:T(8,128)(2,1)} %get-tuple-element.21, bf16[8,192,2048,1]{2,1,3,0:T(8,128)(2,1)} %bitcast.60), kind=kOutput, calls=%fused_computation.23 | convolution fusion | flops 12884901888 | bytes 29360128 | tf_op jit(solution)/shard_map/bte,bhtd->hed/dot_general | solution.py:337
  354.9 0.3 reduce-scatter.8.cloned.1.call-start
  355.3 20.6 %convolution_bitcast_fusion = f32[8,256,2048]{2,1,0:T(8,128)} fusion(bf16[8,8,192,256]{3,2,1,0:T(8,128)(2,1)} %get-tuple-element.19, bf16[8,192,2048]{2,1,0:T(8,128)(2,1)} %param.13), kind=kOutput, calls=%fused_computation.22 | convolution fusion | flops 12884901888 | bytes 29360128 | tf_op jit(solution)/shard_map/bhtd,bte->hde/dot_general | solution.py:335
  375.9 0.6 copy-done.5
  376.5 3.8 convert_reduce_fusion
  380.3 4.7 fusion.11
  385.0 21.0 %fusion.12 = bf16[8,192,2048]{2,1,0:T(8,128)(2,1)} fusion(bf16[8,192,2048]{2,1,0:T(8,128)(2,1)} %param.7, bf16[8,8,192,256]{3,2,1,0:T(8,128)(2,1)} %get-tuple-element.19, bf16[8,256,2048]{2,1,0:T(8,128)(2,1)} %get-tuple-element.20), kind=kOutput, calls=%fused_computation.15 | convolution fusion | flops 12894339072 | bytes 27262976 | tf_op jit(solution)/shard_map/bhtd,hde->bte/dot_general | solution.py:339
  406.0 6.5 %fusion.22 = f32[8,192,2048]{2,1,0:T(8,128)} fusion(bf16[2048,512]{1,0:T(8,128)(2,1)S(1)} %copy-done.3, bf16[8,192,256]{2,1,0:T(8,128)(2,1)S(1)} %get-tuple-element.40, bf16[8,192,128]{2,1,0:T(8,128)(2,1)S(1)} %get-tuple-element.38, bf16[8,192,128]{2,1,0:T(8,128)(2,1)S(1)} %get-tuple-element.37), kind=kOutput, calls=%fused_computation.26 | convolution fusion | flops 3225944064 | bytes 16252928 | tf_op jit(solution)/shard_map/btd,ed->bte/dot_general | solution.py:346
  412.5 26.3 %fusion.10 = (f32[2048]{0:T(1024)S(1)}, f32[8,192]{1,0:T(8,128)S(1)}, f32[8,192]{1,0:T(8,128)S(1)}, f32[8,192,2048]{2,1,0:T(8,128)}) fusion(bf16[8,192,2048]{2,1,0:T(8,128)(2,1)} %param.7, f32[8,192]{1,0:T(8,128)S(1)} %add_rsqrt_fusion, f32[8,192]{1,0:T(8,128)S(1)} %broadcast_multiply_fusion.2, f32[2048]{0:T(1024)S(1)} %convert_element_type.42, ...), kind=kOutput, calls=%fused_computation.13 | convolution fusion | flops 12916353024 | bytes 46178304 | tf_op jit(solution)/shard_map/bhtd,hed->bte/dot_general | solution.py:345
  438.8 13.9 %psum.14 = f32[2048]{0:T(1024)} all-reduce(f32[2048]{0:T(1024)S(1)} %get-tuple-element.32), channel_id=1, replica_groups=mesh['dp'=2,'tp'=8] {'tp'}, use_global_device_ids=true, to_apply=%region_6.0 | all-reduce | flops 2048 | bytes 16384 | tf_op jit(solution)/shard_map/psum | solution.py:348
  452.7 13.6 %fusion.9 = bf16[8,192,2048]{2,1,0:T(8,128)(2,1)} fusion(bf16[8,192,2048]{2,1,0:T(8,128)(2,1)} %param.7, bf16[8,192,2048]{2,1,0:T(8,128)(2,1)} %param.13, f32[8,192,2048]{2,1,0:T(8,128)} %get-tuple-element.44, f32[8,192]{1,0:T(8,128)S(1)} %get-tuple-element.45, f32[8,192]{1,0:T(8,128)S(1)} %get-tuple-element.46, f32[2048]{0:T(1024)S(1)} %convert_element_type.42, ...), kind=kLoop, calls=%fused_computation.12 | loop fusion | flops 34603008 | bytes 31490048 | tf_op jit(solution)/shard_map/convert_element_type | solution.py:350
  466.3 4.6 fusion.27
  470.9 17.5 %reduce-scatter.6.cloned.1.call-done = f32[1,2048,256]{1,2,0:T(8,128)} async-done(((f32[8,2048,256]{1,2,0:T(8,128)}), f32[1,2048,256]{1,2,0:T(8,128)}) %reduce-scatter.6.cloned.1.call-update) | async-done | bytes 2097168 | tf_op jit(solution)/shard_map/reduce_scatter | solution.py:338
  488.4 1.7 convert_bitcast_fusion.1
  490.1 1.3 copy.16
  491.4 86.4 %reduce-scatter.8.cloned.1.call-done = f32[1,256,2048]{2,1,0:T(8,128)} async-done(((f32[8,256,2048]{2,1,0:T(8,128)}), f32[1,256,2048]{2,1,0:T(8,128)}) %reduce-scatter.8.cloned.1.call-update) | async-done | bytes 2097168 | tf_op jit(solution)/shard_map/reduce_scatter | solution.py:336
  577.9 2.7 convert_bitcast_fusion
  (25 shorter events, 0.5 us)
Async XLA Ops:
  7.2 151.7 %all-gather.2.cloned.1.call-start = ((), (), s32[]{:S(2)}) async-start(), calls=%async_computation.3 | async-start | bytes 14155776 | tf_op jit(solution)/shard_map/all_gather | solution.py:325
  10.3 83.8 %copy-start = (f32[192,128]{1,0:T(8,128)}, f32[192,128]{1,0:T(8,128)S(1)}, u32[]{:S(2)}) copy-start(f32[192,128]{1,0:T(8,128)S(1)} %get-tuple-element.43.cos_ref) | copy-start | bytes 294916
  10.3 83.8 %copy-start.4 = (f32[192,128]{1,0:T(8,128)}, f32[192,128]{1,0:T(8,128)S(1)}, u32[]{:S(2)}) copy-start(f32[192,128]{1,0:T(8,128)S(1)} %get-tuple-element.42.sin_ref) | copy-start | bytes 294916
  11.7 1.5 copy-start.2
  94.2 229.7 %reduce-scatter.4.cloned.1.call-start = ((), (), s32[]{:S(2)}) async-start(), calls=%async_computation.4 | async-start | bytes 14155776 | tf_op jit(solution)/shard_map/reduce_scatter | solution.py:334
  255.1 70.5 %copy-start.1 = (f32[192,128]{1,0:T(8,128)S(1)}, f32[192,128]{1,0:T(8,128)}, u32[]{:S(2)}) copy-start(f32[192,128]{1,0:T(8,128)} %copy-done) | copy-start | bytes 294916
  255.1 211.1 %all-reduce.2.cloned.1.call-start = ((), (), s32[]{:S(2)}) async-start(), calls=%async_computation.6 | async-start | bytes 8388608 | tf_op jit(solution)/shard_map/psum | solution.py:344
  334.1 154.3 %reduce-scatter.6.cloned.1.call-start = ((), (), s32[]{:S(2)}) async-start(), calls=%async_computation.5 | async-start | bytes 18874368 | tf_op jit(solution)/shard_map/reduce_scatter | solution.py:338
  354.9 222.9 %reduce-scatter.8.cloned.1.call-start = ((), (), s32[]{:S(2)}) async-start(), calls=%async_computation.7 | async-start | bytes 18874368 | tf_op jit(solution)/shard_map/reduce_scatter | solution.py:336
  375.8 0.7 copy-start.5
  385.0 21.0 %copy-start.3 = (bf16[2048,512]{1,0:T(8,128)(2,1)S(1)}, bf16[2048,512]{1,0:T(8,128)(2,1)}, u32[]{:S(2)}) copy-start(bf16[2048,512]{1,0:T(8,128)(2,1)} %copy-done.2) | copy-start | bytes 6291460
Sparse Core Ops, SparseCore 0:
  94.4 64.4 all-gather.1
  255.3 68.6 reduce-scatter.3
  334.2 63.7 all-reduce.1
  400.2 88.1 reduce-scatter.5
  490.6 87.2 reduce-scatter.7
where the time goes:
time: 595 us; the launch traced here: 587 us
  waiting for transfers between devices  237 us (40%)
  Pallas kernels  177 us (30%)
  matrix products  103 us (17%)
  other arithmetic  28.7 us (5%)
  between operations  14.1 us (2%)
  blocking collectives  13.9 us (2%)
  local copies, waits for them, and re-layouts  12 us (2%)
    pallas_call x1, Pallas kernels, attention(): pl.pallas_call(functools.partial(attn_body, n_heads, tok, seq, d, group),...  96.2 us
    reduce_scatter x1, waiting for transfers between devices, device_step(): lax.psum_scatter(gwo, 'tp', scatter_dimension=0, tiled=True)[0].astype(BF16)  86.4 us
    pallas_call x1, Pallas kernels, project(): pl.pallas_call(functools.partial(proj_body, nb, tok), in_specs=[any_spec,...  80.9 us
    reduce_scatter x1, waiting for transfers between devices, device_step(): dkv_loc = lax.psum_scatter(dkv, 'tp', scatter_dimension=1, tiled=True)  68.5 us
    all_gather x1, waiting for transfers between devices, device_step(): kv_full = lax.all_gather(kv_loc, 'tp', axis=1, tiled=True)  64.3 us
    dot_general x1, matrix products, device_step(): dhn = jnp.einsum('bhtd,hed->bte', dq, wq_h, preferred_element_type=F32)  26.3 us
    dot_general x1, matrix products, device_step(): jnp.einsum('bhtd,hde->bte', o, wo_h, preferred_element_type=F32)  21 us
    dot_general x1, matrix products, device_step(): gwq = jnp.einsum('bte,bhtd->hed', hn, dq, preferred_element_type=F32)  20.7 us
  transfers between devices with their start and end apart: 5, of which 4 were waited for; matrix products, arithmetic and copies ran while one was open for 21% of the time, Pallas kernels for 0%

commit v1 on v0

--- a/solution.py
+++ b/solution.py
@@ -35,86 +35,6 @@
     return lax.dot_general(a, b, (((1,), (1,)), ((), ())), preferred_element_type=F32)
 
 
-def attn_body(n_heads, tok, seq, d, group, q_ref, do_ref, kv_ref, cos_ref, sin_ref,
-              o_ref, dq_ref, dkv_ref, bias, s_buf, p_buf, ds_buf):
-    scale = d ** -0.5
-    rows = group * tok
-    kb = 256
-    half = d // 2
-
-    @pl.when(pl.program_id(0) == 0)
-    def _():
-        t0 = lax.axis_index('tp') * tok
-        row = lax.broadcasted_iota(jnp.int32, (tok, seq), 0) + t0
-        col = lax.broadcasted_iota(jnp.int32, (tok, seq), 1)
-        bias[...] = jnp.where(col <= row, F32(3.0e38), F32(-1e30))
-
-    for g in range(n_heads // group):
-        q = jnp.concatenate([q_ref[0, g * group + j] for j in range(group)], axis=0)
-        do = jnp.concatenate([do_ref[0, g * group + j] for j in range(group)], axis=0)
-        for c in range(seq // kb):
-            cols = slice(c * kb, (c + 1) * kb)
-            s_buf[:, cols] = dot_nt(q, kv_ref[0, cols, :d])
-        rb = 16
-        for r in range(rows // rb):
-            rs = slice(r * rb, (r + 1) * rb)
-            t = (r * rb) % tok
-            s = jnp.minimum(s_buf[rs, :], bias[t:t + rb, :])
-            m = jnp.max(s, axis=1, keepdims=True)
-            e = jnp.exp2(s * (scale * LOG2E) - m * (scale * LOG2E))
-            l = jnp.sum(e, axis=1, keepdims=True)
-            p_buf[rs, :] = (e * (1.0 / l)).astype(BF16)
-        o = dot_nn(p_buf[...], kv_ref[0, :, d:])
-        dvec = jnp.sum(o * do.astype(F32), axis=1, keepdims=True)
-        o16 = o.astype(BF16)
-        for j in range(group):
-            o_ref[0, g * group + j] = o16[j * tok:(j + 1) * tok]
-        dv_t = dot_nn(do.T, p_buf[...])
-        for c in range(seq // kb):
-            cols = slice(c * kb, (c + 1) * kb)
-            dp = dot_nt(do, kv_ref[0, cols, d:])
-            ds_buf[:, cols] = (p_buf[:, cols].astype(F32) * (dp - dvec)).astype(BF16)
-        dq = dot_nn(ds_buf[...], kv_ref[0, :, :d]) * scale
-        dk_t = dot_nn(q.T, ds_buf[...])
-        for j in range(group):
-            part = dq[j * tok:(j + 1) * tok]
-            lo, hi = part[:, :half], part[:, half:]
-            cs, sn = cos_ref[...], sin_ref[...]
-            dq_ref[0, g * group + j, :, :half] = (lo * cs + hi * sn).astype(BF16)
-            dq_ref[0, g * group + j, :, half:] = (hi * cs - lo * sn).astype(BF16)
-        if g == 0:
-            dk_acc, dv_acc = dk_t, dv_t
-        else:
-            dk_acc = dk_acc + dk_t
-            dv_acc = dv_acc + dv_t
-    dkv_ref[0, :, :d] = (dk_acc * scale).T.astype(BF16)
-    dkv_ref[0, :, d:] = dv_acc.T.astype(BF16)
-
-
-def attention(q, do, kv, cos_t, sin_t):
-    n_batch, n_heads, tok, d = q.shape
-    seq = kv.shape[1]
-    group = 4
-    rows = group * tok
-    head_spec = pl.BlockSpec((1, n_heads, tok, d), lambda b: (b, 0, 0, 0))
-    kv_spec = pl.BlockSpec((1, seq, 2 * d), lambda b: (b, 0, 0))
-    tab_spec = pl.BlockSpec((tok, d // 2), lambda b: (0, 0))
-    return pl.pallas_call(
-        functools.partial(attn_body, n_heads, tok, seq, d, group),
-        grid=(n_batch,),
-        in_specs=[head_spec, head_spec, kv_spec, tab_spec, tab_spec],
-        out_specs=[head_spec, head_spec, kv_spec],
-        out_shape=[jax.ShapeDtypeStruct(q.shape, BF16), jax.ShapeDtypeStruct(q.shape, BF16),
-                   jax.ShapeDtypeStruct(kv.shape, BF16)],
-        scratch_shapes=[pltpu.VMEM((tok, seq), F32), pltpu.VMEM((rows, seq), F32),
-                        pltpu.VMEM((rows, seq), BF16), pltpu.VMEM((rows, seq), BF16)],
-        compiler_params=pltpu.CompilerParams(dimension_semantics=("arbitrary",), vmem_limit_bytes=56 * 2**20),
-        cost_estimate=pl.CostEstimate(flops=12 * n_batch * n_heads * tok * seq * d, bytes_accessed=40 * 2**20,
-                                      transcendentals=n_batch * n_heads * tok * seq),
-        name="attention",
-    )(q, do, kv, cos_t, sin_t)
-
-
 def rdma(src, dst, send, recv, to):
     return pltpu.make_async_remote_copy(src_ref=src, dst_ref=dst, send_sem=send, recv_sem=recv,
                                         device_id={'tp': to}, device_id_type=pl.DeviceIdType.MESH)
@@ -131,6 +51,299 @@
     for p in peers:
         pl.semaphore_signal(barrier, inc=1, device_id={'tp': p}, device_id_type=pl.DeviceIdType.MESH)
     pl.semaphore_wait(barrier, len(peers))
+
+
+def attn_body(nb, n_heads, tok, seq, d, group, q_hbm, do_hbm, kvl_hbm, cos_ref, sin_ref,
+              o_hbm, dq_hbm, dkv_hbm,
+              kv_all, q_v, do_v, o_v, dq_v, bias, s_buf, p_buf, ds_buf, mrecv, rrecv,
+              kv_send, kv_recv, m_send, m_recv, r_send, r_recv, own_sem, in_sem, out_sem, fin_sem):
+    scale = d ** -0.5
+    rows = group * tok
+    kb = 256
+    half = d // 2
+    me, k, mate, cw, ccw = ring_ids()
+    c = me // 2
+
+    def blk(j):
+        return pl.ds(pl.multiple_of(j * tok, 16), tok)
+
+    def kvb(b, j):
+        return kv_all.at[b, blk(j)]
+
+    def kv_copy(b, j, tag, to, src=None):
+        return rdma(kvb(b, j) if src is None else src, kvb(b, j), kv_send.at[b, tag], kv_recv.at[b, tag], to)
+
+    def own(b):
+        @pl.when(c <= 2)
+        def _():
+            kv_copy(b, me, 0, cw, kvl_hbm.at[b]).start()
+
+        @pl.when(c == 0)
+        def _():
+            kv_copy(b, me, 2, ccw, kvl_hbm.at[b]).start()
+        kv_copy(b, me, 3, mate, kvl_hbm.at[b]).start()
+
+    def service_a(b):
+        @pl.when(c >= 1)
+        def _():
+            kv_copy(b, me - 2, 0, cw).wait_recv()
+
+            @pl.when(c <= 2)
+            def _():
+                kv_copy(b, me - 2, 1, cw).start()
+            kv_copy(b, me - 2, 4, mate).start()
+
+        @pl.when(c == 3)
+        def _():
+            kv_copy(b, me - 6, 2, ccw).wait_recv()
+            kv_copy(b, me - 6, 6, mate).start()
+
+    def service_b(b):
+        @pl.when(c >= 2)
+        def _():
+            kv_copy(b, me - 4, 1, cw).wait_recv()
+            kv_copy(b, me - 4, 5, mate).start()
+
+    def own_copy(b):
+        return pltpu.make_async_copy(kvl_hbm.at[b], kvb(b, me), own_sem.at[b])
+
+    def ready(b):
+        own_copy(b).wait()
+        kv_copy(b, mate, 3, mate).wait_recv()
+        for n, tag in ((1, 4), (2, 5), (3, 6)):
+            @pl.when(c >= n)
+            def _():
+                kv_copy(b, mate - 2 * n, tag, mate).wait_recv()
+
+    def drain_kv(b):
+        for cond, tag in ((c <= 2, 0), ((c >= 1) & (c <= 2), 1), (c == 0, 2), (c >= 0, 3), (c >= 1, 4), (c >= 2, 5), (c == 3, 6)):
+            @pl.when(cond)
+            def _():
+                kv_copy(b, me, tag, mate).wait_send()
+
+    def m_copy(b, n):
+        return rdma(kvb(b, 2 * n + 1 - k), mrecv.at[b, n], m_send.at[b, n], m_recv.at[b, n], mate)
+
+    def r_copy(b, n, slot, to):
+        return rdma(kvb(b, 2 * n + k), rrecv.at[b, slot], r_send.at[b, slot], r_recv.at[b, slot], to)
+
+    def add_into(b, n, other):
+        v = kv_all[b, blk(2 * n + k), :].astype(F32) + other[...].astype(F32)
+        kv_all[b, blk(2 * n + k), :] = v.astype(BF16)
+
+    def fin_copy(b):
+        return pltpu.make_async_copy(kvb(b, me), dkv_hbm.at[b], fin_sem.at[b])
+
+    def to_mate(b):
+        for n in range(4):
+            @pl.when(c >= n)
+            def _():
+                m_copy(b, n).start()
+
+    def stage1(b):
+        for n in range(4):
+            @pl.when(c >= n)
+            def _():
+                m_copy(b, n).wait()
+                add_into(b, n, mrecv.at[b, n])
+
+        @pl.when(c == 3)
+        def _():
+            r_copy(b, 1, 2, ccw).start()
+            r_copy(b, 2, 1, ccw).start()
+            r_copy(b, 0, 0, cw).start()
+            fin_copy(b).start()
+
+        @pl.when(c == 2)
+        def _():
+            r_copy(b, 0, 1, ccw).start()
+
+    def stage2(b):
+        @pl.when(c == 2)
+        def _():
+            r_copy(b, 1, 2, ccw).wait_recv()
+            add_into(b, 1, rrecv.at[b, 2])
+            r_copy(b, 1, 2, ccw).start()
+            r_copy(b, 2, 1, ccw).wait_recv()
+            add_into(b, 2, rrecv.at[b, 1])
+            fin_copy(b).start()
+
+        @pl.when(c == 1)
+        def _():
+            r_copy(b, 0, 1, ccw).wait_recv()
+            add_into(b, 0, rrecv.at[b, 1])
+            r_copy(b, 0, 1, ccw).start()
+
+    def stage3(b):
+        @pl.when(c == 0)
+        def _():
+            r_copy(b, 0, 0, cw).wait_recv()
+            add_into(b, 0, rrecv.at[b, 0])
+            r_copy(b, 0, 1, ccw).wait_recv()
+            add_into(b, 0, rrecv.at[b, 1])
+            fin_copy(b).start()
+
+        @pl.when(c == 1)
+        def _():
+            r_copy(b, 1, 2, ccw).wait_recv()
+            add_into(b, 1, rrecv.at[b, 2])
+            fin_copy(b).start()
+
+    def load(b, slot):
+        return (pltpu.make_async_copy(q_hbm.at[b], q_v.at[slot], in_sem.at[0, slot]),
+                pltpu.make_async_copy(do_hbm.at[b], do_v.at[slot], in_sem.at[1, slot]))
+
+    def store(b, slot):
+        return (pltpu.make_async_copy(o_v.at[slot], o_hbm.at[b], out_sem.at[0, slot]),
+                pltpu.make_async_copy(dq_v.at[slot], dq_hbm.at[b], out_sem.at[1, slot]))
+
+    enter((mate, cw, ccw))
+    for b in range(nb):
+        own_copy(b).start()
+    for x in load(0, 0):
+        x.start()
+    for b in range(min(3, nb)):
+        own(b)
+
+    @pl.loop(2 * c + 2, 8)
+    def _(j):
+        for b in range(nb):
+            kv_all[b, blk(j), :] = jnp.zeros((tok, 2 * d), BF16)
+    t0 = me * tok
+    row = lax.broadcasted_iota(jnp.int32, (tok, seq), 0) + t0
+    col = lax.broadcasted_iota(jnp.int32, (tok, seq), 1)
+    bias[...] = jnp.where(col <= row, F32(3.0e38), F32(-1e30))
+    for b in range(min(2, nb)):
+        service_a(b)
+    service_b(0)
+
+    @pl.loop(0, nb)
+    def _(b):
+        slot = lax.rem(b, 2)
+
+        @pl.when(b + 1 < nb)
+        def _():
+            for x in load(b + 1, 1 - slot):
+                x.start()
+
+        @pl.when(b + 3 < nb)
+        def _():
+            own(b + 3)
+
+        @pl.when(b + 2 < nb)
+        def _():
+            service_a(b + 2)
+
+        @pl.when(b + 1 < nb)
+        def _():
+            service_b(b + 1)
+
+        @pl.when(b >= 1)
+        def _():
+            stage1(b - 1)
+
+        @pl.when(b >= 2)
+        def _():
+            stage2(b - 2)
+            for x in store(b - 2, slot):
+                x.wait()
+
+        @pl.when(b >= 3)
+        def _():
+            stage3(b - 3)
+        for x in load(b, slot):
+            x.wait()
+        ready(b)
+        k_ref = kv_all.at[b, :, :d]
+        v_ref = kv_all.at[b, :, d:]
+        dk_acc = dv_acc = None
+        for g in range(n_heads // group):
+            q = jnp.concatenate([q_v[slot, g * group + j] for j in range(group)], axis=0)
+            do = jnp.concatenate([do_v[slot, g * group + j] for j in range(group)], axis=0)
+            for i in range(seq // kb):
+                cols = slice(i * kb, (i + 1) * kb)
+                s_buf[:, cols] = dot_nt(q, k_ref[cols, :])
+            rb = 16
+            for r in range(rows // rb):
+                rs = slice(r * rb, (r + 1) * rb)
+                t = (r * rb) % tok
+                s = jnp.minimum(s_buf[rs, :], bias[t:t + rb, :])
+                m = jnp.max(s, axis=1, keepdims=True)
+                e = jnp.exp2(s * (scale * LOG2E) - m * (scale * LOG2E))
+                l = jnp.sum(e, axis=1, keepdims=True)
+                p_buf[rs, :] = (e * (1.0 / l)).astype(BF16)
+            o = dot_nn(p_buf[...], v_ref[...])
+            dvec = jnp.sum(o * do.astype(F32), axis=1, keepdims=True)
+            o16 = o.astype(BF16)
+            for j in range(group):
+                o_v[slot, g * group + j] = o16[j * tok:(j + 1) * tok]
+            dv_t = dot_nn(do.T, p_buf[...])
+            for i in range(seq // kb):
+                cols = slice(i * kb, (i + 1) * kb)
+                dp = dot_nt(do, v_ref[cols, :])
+                ds_buf[:, cols] = (p_buf[:, cols].astype(F32) * (dp - dvec)).astype(BF16)
+            dq = dot_nn(ds_buf[...], k_ref[...]) * scale
+            dk_t = dot_nn(q.T, ds_buf[...])
+            for j in range(group):
+                part = dq[j * tok:(j + 1) * tok]
+                lo, hi = part[:, :half], part[:, half:]
+                cs, sn = cos_ref[...], sin_ref[...]
+                dq_v[slot, g * group + j, :, :half] = (lo * cs + hi * sn).astype(BF16)
+                dq_v[slot, g * group + j, :, half:] = (hi * cs - lo * sn).astype(BF16)
+            dk_acc = dk_t if g == 0 else dk_acc + dk_t
+            dv_acc = dv_t if g == 0 else dv_acc + dv_t
+        drain_kv(b)
+        kv_all[b, :, :d] = (dk_acc * scale).T.astype(BF16)
+        kv_all[b, :, d:] = dv_acc.T.astype(BF16)
+        for x in store(b, slot):
+            x.start()
+        to_mate(b)
+
+    n = nb
+    stage1(n - 1)
+    stage2(n - 2)
+    if n >= 3:
+        stage3(n - 3)
+    stage2(n - 1)
+    stage3(n - 2)
+    stage3(n - 1)
+    for b in (n - 2, n - 1):
+        for x in store(b, b % 2):
+            x.wait()
+    for b in range(n):
+        fin_copy(b).wait()
+        for cond, slot in ((c == 3, 0), (c >= 1, 1), (c >= 2, 2)):
+            @pl.when(cond)
+            def _():
+                r_copy(b, 0, slot, cw).wait_send()
+
+
+def attention(q, do, kv, cos_t, sin_t):
+    nb, n_heads, tok, d = q.shape
+    seq = tok * 8
+    group = 4
+    rows = group * tok
+    any_spec = pl.BlockSpec(memory_space=pl.ANY)
+    vmem = pl.BlockSpec(memory_space=pltpu.VMEM)
+    dma = pltpu.SemaphoreType.DMA
+    slab = pltpu.VMEM((2, n_heads, tok, d), BF16)
+    return pl.pallas_call(
+        functools.partial(attn_body, nb, n_heads, tok, seq, d, group),
+        in_specs=[any_spec, any_spec, any_spec, vmem, vmem],
+        out_specs=[any_spec, any_spec, any_spec],
+        out_shape=[jax.ShapeDtypeStruct(q.shape, BF16), jax.ShapeDtypeStruct(q.shape, BF16),
+                   jax.ShapeDtypeStruct(kv.shape, BF16)],
+        scratch_shapes=[pltpu.VMEM((nb, seq, 2 * d), BF16), slab, slab, slab, slab,
+                        pltpu.VMEM((tok, seq), F32), pltpu.VMEM((rows, seq), F32),
+                        pltpu.VMEM((rows, seq), BF16), pltpu.VMEM((rows, seq), BF16),
+                        pltpu.VMEM((nb, 4, tok, 2 * d), BF16), pltpu.VMEM((nb, 3, tok, 2 * d), BF16),
+                        dma((nb, 7)), dma((nb, 7)), dma((nb, 4)), dma((nb, 4)), dma((nb, 3)), dma((nb, 3)),
+                        dma((nb,)), dma((2, 2)), dma((2, 2)), dma((nb,))],
+        compiler_params=pltpu.CompilerParams(collective_id=1, has_side_effects=True, vmem_limit_bytes=63 * 2**20),
+        cost_estimate=pl.CostEstimate(flops=12 * nb * n_heads * tok * seq * d, bytes_accessed=40 * 2**20,
+                                      transcendentals=nb * n_heads * tok * seq),
+        name="attention",
+    )(q, do, kv, cos_t, sin_t)
 
 
 def proj_body(nb, tok, x_hbm, g_ref, wq_hbm, wkv_ref, wo_hbm, dy_hbm, cos_ref, sin_ref,
@@ -322,16 +535,13 @@
 
         w_kv = jnp.concatenate([w_k, w_v], axis=1)
         hn, q, do, kv_loc, wq_h, wo_h = project(x_loc, ln_scale, wq_loc, w_kv, wo_loc, dy_loc, cos_t, sin_t)
-        kv_full = lax.all_gather(kv_loc, 'tp', axis=1, tiled=True)
         x_f32 = x_loc.astype(F32)
         centered = x_f32 - jnp.mean(x_f32, axis=-1, keepdims=True)
         inv_std = lax.rsqrt(jnp.mean(centered * centered, axis=-1, keepdims=True) + LN_EPS)
         x_hat = centered * inv_std
         ln_gain = ln_scale.astype(F32)
 
-        o, dq, dkv = attention(q, do, kv_full, cos_t, sin_t)
-
-        dkv_loc = lax.psum_scatter(dkv, 'tp', scatter_dimension=1, tiled=True)
+        o, dq, dkv_loc = attention(q, do, kv_loc, cos_t, sin_t)
         gwo = jnp.einsum('bhtd,bte->hde', o, dy_loc, preferred_element_type=F32)
         gwo = lax.psum_scatter(gwo, 'tp', scatter_dimension=0, tiled=True)[0].astype(BF16)
         gwq = jnp.einsum('bte,bhtd->hed', hn, dq, preferred_element_type=F32)

time: 595 us -> 521 us (0.88)
  waiting for transfers between devices: 237 us -> 107 us
  Pallas kernels: 177 us -> 234 us
    reduce_scatter x1 -> x0, waiting for transfers between devices: 68.5 us -> none  [device_step(): dkv_loc = lax.psum_scatter(dkv, 'tp', scatter_dimension=1, tiled=True)]
    all_gather x1 -> x0, waiting for transfers between devices: 64.3 us -> none  [device_step(): kv_full = lax.all_gather(kv_loc, 'tp', axis=1, tiled=True)]
    pallas_call x1, Pallas kernels: 96.2 us -> 153 us  [attention(): pl.pallas_call(functools.partial(attn_body, nb, n_heads, tok, seq, d, gro...]
  transfers between devices with their start and end apart: 5 -> 3, of which waited for: 4 -> 2; matrix products, arithmetic and copies ran while one was open for 21% -> 24% of each run, Pallas kernels for 0% -> 0%
where the time goes in v1:
time: 521 us; the launch traced here: 513 us
  Pallas kernels  234 us (45%)
  waiting for transfers between devices  107 us (21%)
  matrix products  100 us (19%)
  other arithmetic  28.9 us (6%)
  blocking collectives  14.4 us (3%)
  between operations  14.4 us (3%)
  local copies, waits for them, and re-layouts  13.4 us (3%)
    pallas_call x1, Pallas kernels, attention(): pl.pallas_call(functools.partial(attn_body, nb, n_heads, tok, seq, d, gro...  153 us
    reduce_scatter x1, waiting for transfers between devices, device_step(): lax.psum_scatter(gwo, 'tp', scatter_dimension=0, tiled=True)[0].astype(BF16)  86.6 us
    pallas_call x1, Pallas kernels, project(): pl.pallas_call(functools.partial(proj_body, nb, tok), in_specs=[any_spec,...  81 us
    dot_general x1, matrix products, device_step(): dhn = jnp.einsum('bhtd,hed->bte', dq, wq_h, preferred_element_type=F32)  26.3 us
    dot_general x1, matrix products, device_step(): gwo = jnp.einsum('bhtd,bte->hde', o, dy_loc, preferred_element_type=F32)  20.7 us
    dot_general x1, matrix products, device_step(): jnp.einsum('bhtd,hde->bte', o, wo_h, preferred_element_type=F32)  20.7 us
    reduce_scatter x1, waiting for transfers between devices, device_step(): lax.psum_scatter(gwq, 'tp', scatter_dimension=0, tiled=True)[0].astype(BF16)  20.5 us
    dot_general x1, matrix products, device_step(): gwq = jnp.einsum('bte,bhtd->hed', hn, dq, preferred_element_type=F32)  20.5 us
  transfers between devices with their start and end apart: 3, of which 2 were waited for; matrix products, arithmetic and copies ran while one was open for 24% of the time, Pallas kernels for 0%

profile of v1, /device:TPU:112, one launch (start us, length us, event | category | flops | bytes accessed | tf_op | source)
XLA Modules:
  0.0 512.7 jit_solution(4610936964066679995)
XLA Ops:
  7.2 0.1 all-reduce.2.cloned.1.call-start
  7.3 1.3 reshape.178.g_ref
  8.6 1.3 constant_dynamic-update-slice_fusion.1
  9.9 1.3 constant_dynamic-update-slice_fusion.wkv_ref
  11.2 0.4 fusion.24
  11.7 1.0 tile.8
  12.6 0.7 tile.20
  13.3 81.0 %project.1 = (bf16[1536,2048]{1,0:T(8,128)(2,1)}, bf16[8,8,192,256]{3,2,1,0:T(8,128)(2,1)}, bf16[8,8,192,256]{3,2,1,0:T(8,128)(2,1)}, bf16[1536,512]{1,0:T(8,128...) custom-call(bf16[1536,2048]{1,0:T(8,128)(2,1)} %bitcast.54, bf16[1,2048]{1,0:T(2,128)(2,1)} %reshape.178.g_ref, ...), custom_call_target="tpu_custom_call" | custom-call | flops 28991029248 | bytes 62914560 | tf_op jit(solution)/shard_map/project/pallas_call | solution.py:510
  94.3 152.8 %attention.1 = (bf16[8,8,192,256]{3,2,1,0:T(8,128)(2,1)}, bf16[8,8,192,256]{3,2,1,0:T(8,128)(2,1)}, bf16[8,192,512]{2,1,0:T(8,128)(2,1)}) custom-call(bf16[8,8,192,256]{3,2,1,0:T(8,128)(2,1)} %get-tuple-element.16.q_hbm, bf16[8,8,192,256]{3,2,1,0:T(8,128)(2,1)} %get-tuple-element.17.do_hbm, bf16[8,192,512]{2,1,0:T(8,128)(2,1)} %bitcast.60, ...), custom_call_target="tpu_custom_call" | custom-call | flops 57982058496 | bytes 41943040 | tf_op jit(solution)/shard_map/attention/pallas_call | solution.py:330
  247.2 1.7 slice_convert_fusion
  248.9 0.2 subtract_convert_fusion
  249.1 1.3 copy-done.6
  250.4 5.4 %convolution_bitcast_fusion.2 = f32[2048,512]{1,0:T(8,128)} fusion(bf16[8,192,2048]{2,1,0:T(8,128)(2,1)S(1)} %bitcast.59, bf16[8,192,256]{2,1,0:T(8,128)(2,1)S(1)} %get-tuple-element.40, bf16[8,192,128]{2,1,0:T(8,128)(2,1)S(1)} %get-tuple-element.38, bf16[8,192,128]{2,1,0:T(8,128)(2,1)S(1)} %get-tuple-element.37), kind=kOutput, calls=%fused_computation.25 | convolution fusion | flops 3225944064 | bytes 12058624 | tf_op jit(solution)/shard_map/bte,btd->ed/dot_general | solution.py:553
  255.9 0.1 reduce-scatter.3.cloned.1.call-start
  256.0 20.5 %convolution_bitcast_fusion.1 = f32[8,2048,256]{1,2,0:T(8,128)} fusion(bf16[8,8,192,256]{3,2,1,0:T(8,128)(2,1)} %get-tuple-element.21, bf16[8,192,2048,1]{2,1,3,0:T(8,128)(2,1)} %bitcast.58), kind=kOutput, calls=%fused_computation.23 | convolution fusion | flops 12884901888 | bytes 29360128 | tf_op jit(solution)/shard_map/bte,bhtd->hed/dot_general | solution.py:547
  276.4 0.1 reduce-scatter.3.cloned.1.call-update
  276.5 0.2 reduce-scatter.5.cloned.1.call-start
  276.7 20.7 %convolution_bitcast_fusion = f32[8,256,2048]{2,1,0:T(8,128)} fusion(bf16[8,8,192,256]{3,2,1,0:T(8,128)(2,1)} %get-tuple-element.19, bf16[8,192,2048]{2,1,0:T(8,128)(2,1)} %param.13), kind=kOutput, calls=%fused_computation.22 | convolution fusion | flops 12884901888 | bytes 29360128 | tf_op jit(solution)/shard_map/bhtd,bte->hde/dot_general | solution.py:545
  297.5 0.6 copy-done.5
  298.2 3.8 convert_reduce_fusion
  302.0 4.7 fusion.11
  306.7 6.6 %fusion.22 = f32[8,192,2048]{2,1,0:T(8,128)} fusion(bf16[2048,512]{1,0:T(8,128)(2,1)S(1)} %copy-done.3, bf16[8,192,256]{2,1,0:T(8,128)(2,1)S(1)} %get-tuple-element.40, bf16[8,192,128]{2,1,0:T(8,128)(2,1)S(1)} %get-tuple-element.38, bf16[8,192,128]{2,1,0:T(8,128)(2,1)S(1)} %get-tuple-element.37), kind=kOutput, calls=%fused_computation.26 | convolution fusion | flops 3225944064 | bytes 16252928 | tf_op jit(solution)/shard_map/btd,ed->bte/dot_general | solution.py:556
  313.3 26.3 %fusion.10 = (f32[2048]{0:T(1024)S(1)}, f32[8,192]{1,0:T(8,128)S(1)}, f32[8,192]{1,0:T(8,128)S(1)}, f32[8,192,2048]{2,1,0:T(8,128)}) fusion(bf16[8,192,2048]{2,1,0:T(8,128)(2,1)} %param.7, f32[8,192]{1,0:T(8,128)S(1)} %add_rsqrt_fusion, f32[8,192]{1,0:T(8,128)S(1)} %broadcast_multiply_fusion.2, f32[2048]{0:T(1024)S(1)} %convert_element_type.42, ...), kind=kOutput, calls=%fused_computation.13 | convolution fusion | flops 12916353024 | bytes 46178304 | tf_op jit(solution)/shard_map/bhtd,hed->bte/dot_general | solution.py:555
  339.6 14.4 %psum.14 = f32[2048]{0:T(1024)} all-reduce(f32[2048]{0:T(1024)S(1)} %get-tuple-element.32), channel_id=1, replica_groups=mesh['dp'=2,'tp'=8] {'tp'}, use_global_device_ids=true, to_apply=%region_5.0 | all-reduce | flops 2048 | bytes 16384 | tf_op jit(solution)/shard_map/psum | solution.py:558
  354.0 13.6 %fusion.9 = bf16[8,192,2048]{2,1,0:T(8,128)(2,1)} fusion(bf16[8,192,2048]{2,1,0:T(8,128)(2,1)} %param.7, bf16[8,192,2048]{2,1,0:T(8,128)(2,1)} %param.13, f32[8,192,2048]{2,1,0:T(8,128)} %get-tuple-element.44, f32[8,192]{1,0:T(8,128)S(1)} %get-tuple-element.45, f32[8,192]{1,0:T(8,128)S(1)} %get-tuple-element.46, f32[2048]{0:T(1024)S(1)} %convert_element_type.42, ...), kind=kLoop, calls=%fused_computation.12 | loop fusion | flops 34603008 | bytes 31490048 | tf_op jit(solution)/shard_map/convert_element_type | solution.py:560
  367.5 20.7 %fusion.12 = bf16[8,192,2048]{2,1,0:T(8,128)(2,1)} fusion(bf16[8,192,2048]{2,1,0:T(8,128)(2,1)} %param.7, bf16[8,8,192,256]{3,2,1,0:T(8,128)(2,1)} %get-tuple-element.19, bf16[8,256,2048]{2,1,0:T(8,128)(2,1)} %get-tuple-element.20), kind=kOutput, calls=%fused_computation.15 | convolution fusion | flops 12894339072 | bytes 27262976 | tf_op jit(solution)/shard_map/bhtd,hde->bte/dot_general | solution.py:549
  388.2 4.6 fusion.27
  392.8 20.5 %reduce-scatter.3.cloned.1.call-done = f32[1,2048,256]{1,2,0:T(8,128)} async-done(((f32[8,2048,256]{1,2,0:T(8,128)}), f32[1,2048,256]{1,2,0:T(8,128)}) %reduce-scatter.3.cloned.1.call-update) | async-done | bytes 2097168 | tf_op jit(solution)/shard_map/reduce_scatter | solution.py:548
  413.3 1.7 convert_bitcast_fusion.1
  415.1 1.3 copy.16
  416.4 86.6 %reduce-scatter.5.cloned.1.call-done = f32[1,256,2048]{2,1,0:T(8,128)} async-done(((f32[8,256,2048]{2,1,0:T(8,128)}), f32[1,256,2048]{2,1,0:T(8,128)}) %reduce-scatter.5.cloned.1.call-update) | async-done | bytes 2097168 | tf_op jit(solution)/shard_map/reduce_scatter | solution.py:546
  503.0 2.7 convert_bitcast_fusion
  (21 shorter events, 0.2 us)
Async XLA Ops:
  7.2 381.1 %all-reduce.2.cloned.1.call-start = ((), (), s32[]{:S(2)}) async-start(), calls=%async_computation.3 | async-start | bytes 8388608 | tf_op jit(solution)/shard_map/psum | solution.py:554
  11.2 2.1 copy-start.2
  11.6 82.7 %copy-start = (f32[192,128]{1,0:T(8,128)}, f32[192,128]{1,0:T(8,128)S(1)}, u32[]{:S(2)}) copy-start(f32[192,128]{1,0:T(8,128)S(1)} %get-tuple-element.43.cos_ref) | copy-start | bytes 294916
  11.6 82.7 %copy-start.4 = (f32[192,128]{1,0:T(8,128)}, f32[192,128]{1,0:T(8,128)S(1)}, u32[]{:S(2)}) copy-start(f32[192,128]{1,0:T(8,128)S(1)} %get-tuple-element.42.sin_ref) | copy-start | bytes 294916
  94.3 154.6 %copy-start.1 = (f32[192,128]{1,0:T(8,128)S(1)}, f32[192,128]{1,0:T(8,128)}, u32[]{:S(2)}) copy-start(f32[192,128]{1,0:T(8,128)} %copy-done) | copy-start | bytes 294916
  247.2 3.3 copy-start.6
  255.9 157.5 %reduce-scatter.3.cloned.1.call-start = ((), (), s32[]{:S(2)}) async-start(), calls=%async_computation.2 | async-start | bytes 18874368 | tf_op jit(solution)/shard_map/reduce_scatter | solution.py:548
  276.5 226.5 %reduce-scatter.5.cloned.1.call-start = ((), (), s32[]{:S(2)}) async-start(), calls=%async_computation.4 | async-start | bytes 18874368 | tf_op jit(solution)/shard_map/reduce_scatter | solution.py:546
  297.5 0.7 copy-start.5
  298.2 8.6 %copy-start.3 = (bf16[2048,512]{1,0:T(8,128)(2,1)S(1)}, bf16[2048,512]{1,0:T(8,128)(2,1)}, u32[]{:S(2)}) copy-start(bf16[2048,512]{1,0:T(8,128)(2,1)} %copy-done.2) | copy-start | bytes 6291460
Sparse Core Ops, SparseCore 0:
  256.0 66.7 all-reduce.1
  325.2 88.1 reduce-scatter.2
  415.7 87.2 reduce-scatter.4

commit v2 on v1

--- a/solution.py
+++ b/solution.py
@@ -54,9 +54,9 @@
 
 
 def attn_body(nb, n_heads, tok, seq, d, group, q_hbm, do_hbm, kvl_hbm, cos_ref, sin_ref,
-              o_hbm, dq_hbm, dkv_hbm,
+              o_hbm, dq_hbm, dkv_hbm, op_hbm, dqp_hbm,
               kv_all, q_v, do_v, o_v, dq_v, bias, s_buf, p_buf, ds_buf, mrecv, rrecv,
-              kv_send, kv_recv, m_send, m_recv, r_send, r_recv, own_sem, in_sem, out_sem, fin_sem):
+              kv_send, kv_recv, m_send, m_recv, r_send, r_recv, own_sem, in_sem, out_sem, fin_sem, p_send, p_recv):
     scale = d ** -0.5
     rows = group * tok
     kb = 256
@@ -196,6 +196,10 @@
     def store(b, slot):
         return (pltpu.make_async_copy(o_v.at[slot], o_hbm.at[b], out_sem.at[0, slot]),
                 pltpu.make_async_copy(dq_v.at[slot], dq_hbm.at[b], out_sem.at[1, slot]))
+
+    def hand(b, slot):
+        return (rdma(o_v.at[slot, 1 - k], op_hbm.at[b], p_send.at[0, b], p_recv.at[0, b], mate),
+                rdma(dq_v.at[slot, 1 - k], dqp_hbm.at[b], p_send.at[1, b], p_recv.at[1, b], mate))
 
     enter((mate, cw, ccw))
     for b in range(nb):
@@ -247,6 +251,8 @@
             stage2(b - 2)
             for x in store(b - 2, slot):
                 x.wait()
+            for x in hand(b - 2, slot):
+                x.wait_send()
 
         @pl.when(b >= 3)
         def _():
@@ -276,7 +282,7 @@
             dvec = jnp.sum(o * do.astype(F32), axis=1, keepdims=True)
             o16 = o.astype(BF16)
             for j in range(group):
-                o_v[slot, g * group + j] = o16[j * tok:(j + 1) * tok]
+                o_v[slot, j % 2, (g * group + j) // 2] = o16[j * tok:(j + 1) * tok]
             dv_t = dot_nn(do.T, p_buf[...])
             for i in range(seq // kb):
                 cols = slice(i * kb, (i + 1) * kb)
@@ -288,14 +294,14 @@
                 part = dq[j * tok:(j + 1) * tok]
                 lo, hi = part[:, :half], part[:, half:]
                 cs, sn = cos_ref[...], sin_ref[...]
-                dq_v[slot, g * group + j, :, :half] = (lo * cs + hi * sn).astype(BF16)
-                dq_v[slot, g * group + j, :, half:] = (hi * cs - lo * sn).astype(BF16)
+                dq_v[slot, j % 2, (g * group + j) // 2, :, :half] = (lo * cs + hi * sn).astype(BF16)
+                dq_v[slot, j % 2, (g * group + j) // 2, :, half:] = (hi * cs - lo * sn).astype(BF16)
             dk_acc = dk_t if g == 0 else dk_acc + dk_t
             dv_acc = dv_t if g == 0 else dv_acc + dv_t
         drain_kv(b)
         kv_all[b, :, :d] = (dk_acc * scale).T.astype(BF16)
         kv_all[b, :, d:] = dv_acc.T.astype(BF16)
-        for x in store(b, slot):
+        for x in store(b, slot) + hand(b, slot):
             x.start()
         to_mate(b)
 
@@ -310,7 +316,11 @@
     for b in (n - 2, n - 1):
         for x in store(b, b % 2):
             x.wait()
+        for x in hand(b, b % 2):
+            x.wait_send()
     for b in range(n):
+        for x in hand(b, b % 2):
+            x.wait_recv()
         fin_copy(b).wait()
         for cond, slot in ((c == 3, 0), (c >= 1, 1), (c >= 2, 2)):
             @pl.when(cond)
@@ -327,18 +337,20 @@
     vmem = pl.BlockSpec(memory_space=pltpu.VMEM)
     dma = pltpu.SemaphoreType.DMA
     slab = pltpu.VMEM((2, n_heads, tok, d), BF16)
+    oslab = pltpu.VMEM((2, 2, n_heads // 2, tok, d), BF16)
+    out = jax.ShapeDtypeStruct((nb, 2, n_heads // 2, tok, d), BF16)
+    outp = jax.ShapeDtypeStruct((nb, n_heads // 2, tok, d), BF16)
     return pl.pallas_call(
         functools.partial(attn_body, nb, n_heads, tok, seq, d, group),
         in_specs=[any_spec, any_spec, any_spec, vmem, vmem],
-        out_specs=[any_spec, any_spec, any_spec],
-        out_shape=[jax.ShapeDtypeStruct(q.shape, BF16), jax.ShapeDtypeStruct(q.shape, BF16),
-                   jax.ShapeDtypeStruct(kv.shape, BF16)],
-        scratch_shapes=[pltpu.VMEM((nb, seq, 2 * d), BF16), slab, slab, slab, slab,
+        out_specs=[any_spec] * 5,
+        out_shape=[out, out, jax.ShapeDtypeStruct(kv.shape, BF16), outp, outp],
+        scratch_shapes=[pltpu.VMEM((nb, seq, 2 * d), BF16), slab, slab, oslab, oslab,
                         pltpu.VMEM((tok, seq), F32), pltpu.VMEM((rows, seq), F32),
                         pltpu.VMEM((rows, seq), BF16), pltpu.VMEM((rows, seq), BF16),
                         pltpu.VMEM((nb, 4, tok, 2 * d), BF16), pltpu.VMEM((nb, 3, tok, 2 * d), BF16),
                         dma((nb, 7)), dma((nb, 7)), dma((nb, 4)), dma((nb, 4)), dma((nb, 3)), dma((nb, 3)),
-                        dma((nb,)), dma((2, 2)), dma((2, 2)), dma((nb,))],
+                        dma((nb,)), dma((2, 2)), dma((2, 2)), dma((nb,)), dma((2, nb)), dma((2, nb))],
         compiler_params=pltpu.CompilerParams(collective_id=1, has_side_effects=True, vmem_limit_bytes=63 * 2**20),
         cost_estimate=pl.CostEstimate(flops=12 * nb * n_heads * tok * seq * d, bytes_accessed=40 * 2**20,
                                       transcendentals=nb * n_heads * tok * seq),
@@ -347,9 +359,9 @@
 
 
 def proj_body(nb, tok, x_hbm, g_ref, wq_hbm, wkv_ref, wo_hbm, dy_hbm, cos_ref, sin_ref,
-              hn_hbm, q_hbm, do_hbm, kv_hbm, wqf_hbm, wof_hbm,
+              hn_hbm, q_hbm, do_hbm, kv_hbm, wqf_hbm, wof_hbm, hnp_hbm, dyp_hbm,
               x_v, hn_v, dy_v, wq_v, wo_v, kv_v, out_v,
-              send, recv, x_sem, dy_sem, own_sem, out_sem, misc_sem, w_sem):
+              send, recv, x_sem, dy_sem, own_sem, out_sem, misc_sem, w_sem, p_send, p_recv):
     n_tok, e = x_hbm.shape
     d = kv_v.shape[1] // 2
     half = d // 2
@@ -414,6 +426,9 @@
             hn_v[rs, :] = (c * inv * gain).astype(BF16)
     hn_out = pltpu.make_async_copy(hn_v, hn_hbm, misc_sem.at[0])
     hn_out.start()
+    to_mate = [rdma(hn_v, hnp_hbm, p_send.at[0], p_recv.at[0], mate), rdma(dy_hbm, dyp_hbm, p_send.at[1], p_recv.at[1], mate)]
+    for c in to_mate:
+        c.start()
 
     def rope_rows(raw):
         lo, hi = raw[:, :half], raw[:, half:d]
@@ -494,6 +509,8 @@
         c.wait()
     for c in sends:
         c.wait_send()
+    for c in to_mate:
+        c.wait()
 
 
 def project(x, gain, wq, w_kv, wo, dy, cos_t, sin_t):
@@ -507,21 +524,355 @@
     dma = pltpu.SemaphoreType.DMA
     flops = 2 * n_tok * e * (2 * n_heads + 2) * d
     cos2, sin2 = jnp.tile(cos_t, (2, 1)), jnp.tile(sin_t, (2, 1))
-    hn, q, do, kv, wqf, wof = pl.pallas_call(
+    hn, q, do, kv, wqf, wof, hn_p, dy_p = pl.pallas_call(
         functools.partial(proj_body, nb, tok),
         in_specs=[any_spec, vmem, any_spec, vmem, any_spec, any_spec, vmem, vmem],
-        out_specs=[any_spec] * 6,
+        out_specs=[any_spec] * 8,
         out_shape=[jax.ShapeDtypeStruct((n_tok, e), BF16), act, act, jax.ShapeDtypeStruct((n_tok, 2 * d), BF16),
-                   jax.ShapeDtypeStruct((n_heads, e, d), BF16), jax.ShapeDtypeStruct((n_heads, d, e), BF16)],
+                   jax.ShapeDtypeStruct((n_heads, e, d), BF16), jax.ShapeDtypeStruct((n_heads, d, e), BF16),
+                   jax.ShapeDtypeStruct((n_tok, e), BF16), jax.ShapeDtypeStruct((n_tok, e), BF16)],
         scratch_shapes=[pltpu.VMEM((n_tok, e), BF16), pltpu.VMEM((n_tok, e), BF16), pltpu.VMEM((n_tok, e), BF16),
                         pltpu.VMEM((n_heads, e, d), BF16), pltpu.VMEM((n_heads, d, e), BF16),
                         pltpu.VMEM((n_tok, 2 * d), BF16), pltpu.VMEM((4, nb, tok, d), BF16),
-                        dma((2, 9)), dma((2, 9)), dma((nb,)), dma(()), dma((2,)), dma((4,)), dma((2,)), dma((16,))],
+                        dma((2, 9)), dma((2, 9)), dma((nb,)), dma(()), dma((2,)), dma((4,)), dma((2,)), dma((16,)), dma((2,)), dma((2,))],
         compiler_params=pltpu.CompilerParams(collective_id=0, has_side_effects=True, vmem_limit_bytes=60 * 2**20),
         cost_estimate=pl.CostEstimate(flops=flops, bytes_accessed=60 * 2**20, transcendentals=0),
         name="project",
     )(x.reshape(n_tok, e), gain.reshape(1, e), wq, w_kv, wo, dy.reshape(n_tok, e), cos2, sin2)
-    return hn.reshape(nb, tok, e), q, do, kv.reshape(nb, tok, 2 * d), wqf, wof
+    return hn, q, do, kv.reshape(nb, tok, 2 * d), wqf, wof, hn_p, dy_p
+
+
+def grads_body(nb, tok, o_hbm, op_hbm, dq_hbm, dqp_hbm, hn_hbm, hnp_hbm, dy_hbm, dyp_hbm, dkv_hbm,
+               wq_hbm, wo_hbm, wkv_hbm, x_hbm, g_ref, cos_ref, sin_ref,
+               y_hbm, gx_hbm, gln_ref, gwo_ref, gwq_ref, gkv_hbm,
+               acc, acc_kv, rbuf, rbuf_kv, kind, kp, dkv_v, fin_kv, gln_acc, gl_recv,
+               rs_send, rs_recv, kv_send, kv_recv, ag_send, ag_recv, gl_send, gl_rsem, kp_sem, ld_sem, b_sem, t_sem):
+    n_tok, e = x_hbm.shape
+    d = wkv_hbm.shape[1] // 2
+    half = d // 2
+    eh, eq = e // 2, e // 4
+    me, k, mate, cw, ccw = ring_ids()
+    c = me // 2
+    rel = [lax.rem(c + o, 4) for o in (3, 1, 2, 0)]
+    enter([lax.rem(me + o, 8) for o in range(1, 8)])
+
+    order = ((2, 1), (2, 0))
+
+    def hop(s, dr, j):
+        src = acc.at[s, dr, dr] if j == 0 else rbuf.at[s, dr, j - 1]
+        return rdma(src, rbuf.at[s, dr, j], rs_send.at[s, dr, j], rs_recv.at[s, dr, j], (cw, ccw)[dr])
+
+    def hop_kv(dr, j):
+        src = acc_kv.at[dr, dr] if j == 0 else rbuf_kv.at[dr, j - 1]
+        return rdma(src, rbuf_kv.at[dr, j], kv_send.at[dr, j], kv_recv.at[dr, j], (cw, ccw)[dr])
+
+    def add(dst, term):
+        @pl.loop(0, dst.shape[0] // 32)
+        def _(i):
+            rs = pl.ds(pl.multiple_of(i * 32, 32), 32)
+            dst[rs, :] = dst[rs, :] + term[rs, :]
+
+    def pass_on(s, j):
+        for dr in range(2):
+            hop(s, dr, j - 1).wait_recv()
+            add(rbuf.at[s, dr, j - 1], acc.at[s, order[dr][j - 1], dr])
+            hop(s, dr, j).start()
+
+    def pass_on_kv(j):
+        for dr in range(2):
+            hop_kv(dr, j - 1).wait_recv()
+            add(rbuf_kv.at[dr, j - 1], acc_kv.at[order[dr][j - 1], dr])
+            hop_kv(dr, j).start()
+
+    def finish(s, out):
+        for dr in range(2):
+            hop(s, dr, 2).wait_recv()
+
+            @pl.loop(0, d // 32)
+            def _(i):
+                rs = pl.ds(pl.multiple_of(i * 32, 32), 32)
+                out[rs, dr * eh:(dr + 1) * eh] = (rbuf[s, dr, 2, rs, :] + acc[s, 3, dr, rs, :]).astype(BF16)
+
+    def piece(kk, j, lo=0, n=None):
+        return gkv_hbm.at[kk, pl.ds(lo, d if n is None else n), pl.ds(pl.multiple_of(j * eq, 128), eq)]
+
+    def ag(tag, ref, to, src=None):
+        return rdma(ref if src is None else src, ref, ag_send.at[tag], ag_recv.at[tag], to)
+
+    def ag_far(tag, to):
+        return ag(tag, piece(k, rel[(0, 1)[tag - 3]], (tag - 3) * half, half), to)
+
+    own_piece = pltpu.make_async_copy(fin_kv, piece(k, c), t_sem.at[5])
+
+    def finish_kv():
+        for dr in range(2):
+            hop_kv(dr, 2).wait_recv()
+            fin_kv[:, dr * (eq // 2):(dr + 1) * (eq // 2)] = rbuf_kv[dr, 2] + acc_kv[3, dr]
+        ag(0, piece(k, c), cw, fin_kv).start()
+        ag(1, piece(k, c), ccw, fin_kv).start()
+        ag(2, piece(k, c), mate, fin_kv).start()
+        own_piece.start()
+
+    def ag_forward():
+        ag(0, piece(k, rel[0]), cw).wait_recv()
+        ag_far(3, cw).start()
+        ag(1, piece(k, rel[1]), cw).wait_recv()
+        ag_far(4, ccw).start()
+        ag(5, piece(k, rel[0]), mate).start()
+        ag(6, piece(k, rel[1]), mate).start()
+
+    def ag_last():
+        far = [piece(k, rel[2], i * half, half) for i in range(2)]
+        for i in range(2):
+            ag(3 + i, far[i], cw).wait_recv()
+            ag(7 + i, far[i], mate).start()
+        ag(2, piece(1 - k, c), mate).wait_recv()
+        ag(5, piece(1 - k, rel[0]), mate).wait_recv()
+        ag(6, piece(1 - k, rel[1]), mate).wait_recv()
+        for i in range(2):
+            ag(7 + i, piece(1 - k, rel[2], i * half, half), mate).wait_recv()
+        for tag in range(3):
+            ag(tag, piece(k, c), cw, fin_kv).wait_send()
+        for tag in (3, 4, 7, 8):
+            ag(tag, far[0], cw).wait_send()
+        for tag in (5, 6):
+            ag(tag, piece(k, c), cw).wait_send()
+        own_piece.wait()
+
+    dkv_in = pltpu.make_async_copy(dkv_hbm, dkv_v, t_sem.at[4])
+    dkv_in.start()
+    kp_copy = rdma(kind.at[1 - k], kp, kp_sem.at[0], kp_sem.at[1], mate)
+
+    def products(big, a_v, at):
+        def load_b(own, other):
+            return (pltpu.make_async_copy(own, big.at[0], b_sem.at[0]), pltpu.make_async_copy(other, big.at[1], b_sem.at[1]))
+
+        def load_a(i, own, other, r):
+            return (pltpu.make_async_copy(own.at[:, k, rel[r]], a_v.at[i % 2, 0], ld_sem.at[i % 2, 0]),
+                    pltpu.make_async_copy(other.at[:, rel[r]], a_v.at[i % 2, 1], ld_sem.at[i % 2, 1]))
+
+        def turn(j, src):
+            for i in range(nb // 2):
+                at[j, :, 2 * i * tok:(2 * i + 2) * tok] = jnp.concatenate([src[2 * i], src[2 * i + 1]], axis=0).T
+
+        def both(cols):
+            return dot_nn(at[0], big[0, :, cols]) + dot_nn(at[1], big[1, :, cols])
+
+        hn_in = load_b(hn_hbm, hnp_hbm)
+        for x in hn_in:
+            x.start()
+        jobs = [(1, r) for r in range(4)] + [(0, r) for r in range(4)]
+
+        def fetch(i):
+            s, r = jobs[i]
+            return load_a(i, (o_hbm, dq_hbm)[s], (op_hbm, dqp_hbm)[s], r)
+        for i in range(2):
+            for x in fetch(i):
+                x.start()
+        dkv_in.wait()
+        for b in range(nb):
+            lo, hi = dkv_v[b, :, :half].astype(F32), dkv_v[b, :, half:d].astype(F32)
+            cs, sn = cos_ref[...], sin_ref[...]
+            kind[0, b, :, :half] = (lo * cs + hi * sn).astype(BF16)
+            kind[0, b, :, half:] = (hi * cs - lo * sn).astype(BF16)
+            kind[1, b] = dkv_v[b, :, d:]
+        kp_copy.start()
+        turn(0, kind.at[k])
+        for x in hn_in:
+            x.wait()
+        kp_copy.wait_recv()
+        turn(1, kp)
+        for r in range(4):
+            for dr in range(2):
+                acc_kv[r, dr] = both(pl.ds(pl.multiple_of(rel[r] * eq + dr * (eq // 2), 128), eq // 2))
+        for dr in range(2):
+            hop_kv(dr, 0).start()
+
+        for i, (s, r) in enumerate(jobs):
+            if i == 4:
+                dy_in = load_b(dy_hbm, dyp_hbm)
+                for x in dy_in:
+                    x.start()
+            for x in fetch(i):
+                x.wait()
+            turn(0, a_v.at[i % 2, 0])
+            turn(1, a_v.at[i % 2, 1])
+            if i + 2 < 8:
+                for x in fetch(i + 2):
+                    x.start()
+            if i == 4:
+                for x in dy_in:
+                    x.wait()
+
+            @pl.loop(0, 4)
+            def _(n):
+                cols = pl.ds(pl.multiple_of(n * eq, 128), eq)
+                acc[s, r, n // 2, :, pl.ds(pl.multiple_of(lax.rem(n, 2) * eq, 128), eq)] = both(cols)
+            if r < 2:
+                hop(s, r, 0).start()
+            if i == 1:
+                pass_on_kv(1)
+            if i == 5:
+                pass_on(1, 1)
+                pass_on_kv(2)
+
+    pl.run_scoped(products, pltpu.VMEM((2, n_tok, e), BF16), pltpu.VMEM((2, 2, nb, tok, d), BF16), pltpu.VMEM((2, d, n_tok), BF16))
+
+    mc = 2 * tok
+    units = nb // 2
+
+    def attn_out(wo_v, o_v, x_v, y_v):
+        w_in = pltpu.make_async_copy(wo_hbm, wo_v, b_sem.at[0])
+        w_in.start()
+
+        def load(u):
+            return (pltpu.make_async_copy(o_hbm.at[pl.ds(2 * u, 2)], o_v.at[u % 2], ld_sem.at[u % 2, 0]),
+                    pltpu.make_async_copy(x_hbm.at[pl.ds(u * mc, mc)], x_v.at[u % 2], ld_sem.at[u % 2, 1]))
+
+        def put(u):
+            return pltpu.make_async_copy(y_v.at[u % 2], y_hbm.at[pl.ds(u * mc, mc)], t_sem.at[u % 2])
+        for x in load(0):
+            x.start()
+        w_in.wait()
+        for u in range(units):
+            if u + 1 < units:
+                for x in load(u + 1):
+                    x.start()
+            for x in load(u):
+                x.wait()
+            if u >= 2:
+                put(u - 2).wait()
+            sl = u % 2
+
+            @pl.loop(0, 4)
+            def _(n):
+                cols = pl.ds(pl.multiple_of(n * eq, 128), eq)
+                o_rows = jnp.concatenate([jnp.concatenate([o_v[sl, i, h % 2, h // 2] for h in range(8)], axis=1) for i in range(2)], axis=0)
+                r = dot_nn(o_rows, wo_v[:, cols])
+                y_v[sl, :, cols] = (x_v[sl, :, cols].astype(F32) + r).astype(BF16)
+            put(u).start()
+        for u in range(max(0, units - 2), units):
+            put(u).wait()
+
+    pl.run_scoped(attn_out, pltpu.VMEM((8 * d, e), BF16), pltpu.VMEM((2, 2, 2, 4, tok, d), BF16),
+                  pltpu.VMEM((2, mc, e), BF16), pltpu.VMEM((2, mc, e), BF16))
+    pass_on(0, 1)
+
+    def hidden_grad(wq_v, wkv_v, dq_v, x_v, dy_v, dh, gx_v):
+        w_in = pltpu.make_async_copy(wq_hbm, wq_v, b_sem.at[0])
+        w_in.start()
+        w2_in = pltpu.make_async_copy(wkv_hbm, wkv_v, b_sem.at[1])
+        w2_in.start()
+
+        def load(u):
+            return (pltpu.make_async_copy(dq_hbm.at[pl.ds(2 * u, 2)], dq_v, ld_sem.at[0, 0]),
+                    pltpu.make_async_copy(x_hbm.at[pl.ds(u * mc, mc)], x_v, ld_sem.at[0, 1]),
+                    pltpu.make_async_copy(dy_hbm.at[pl.ds(u * mc, mc)], dy_v, ld_sem.at[1, 0]))
+
+        def put(u):
+            return pltpu.make_async_copy(gx_v, gx_hbm.at[pl.ds(u * mc, mc)], t_sem.at[0])
+        gain = g_ref[...].astype(F32)
+        gln_acc[...] = jnp.zeros_like(gln_acc)
+        for x in load(0):
+            x.start()
+        w_in.wait()
+        w2_in.wait()
+        for u in range(units):
+            for x in load(u):
+                x.wait()
+
+            @pl.loop(0, 4)
+            def _(n):
+                rows = pl.ds(pl.multiple_of(n * eq, 128), eq)
+                t = None
+                for h in range(8):
+                    a = jnp.concatenate([dq_v[i, h % 2, h // 2] for i in range(2)], axis=0)
+                    p = dot_nt(a, wq_v[h, rows, :])
+                    t = p if t is None else t + p
+                for j in range(2):
+                    a = jnp.concatenate([kind[j, 2 * u + i] for i in range(2)], axis=0)
+                    t = t + dot_nt(a, wkv_v[rows, j * d:(j + 1) * d])
+                dh[:, rows] = t
+            if u >= 1:
+                put(u - 1).wait()
+
+            @pl.loop(0, mc // 16)
+            def _(r):
+                rs = pl.ds(pl.multiple_of(r * 16, 16), 16)
+                x = x_v[rs, :].astype(F32)
+                cx = x - jnp.mean(x, axis=1, keepdims=True)
+                inv = lax.rsqrt(jnp.mean(cx * cx, axis=1, keepdims=True) + LN_EPS)
+                xh = cx * inv
+                g = dh[rs, :]
+                pr = g * xh
+                gln_acc[...] += pr[:8] + pr[8:]
+                gh = g * gain
+                m1 = jnp.mean(gh, axis=1, keepdims=True)
+                m2 = jnp.mean(gh * xh, axis=1, keepdims=True)
+                gx_v[rs, :] = (inv * (gh - m1 - xh * m2) + dy_v[rs, :].astype(F32)).astype(BF16)
+            put(u).start()
+            if u + 1 < units:
+                for x in load(u + 1):
+                    x.start()
+            if u == units // 2 - 1:
+                pass_on(1, 2)
+                finish_kv()
+        put(units - 1).wait()
+
+    pl.run_scoped(hidden_grad, pltpu.VMEM((8, e, d), BF16), pltpu.VMEM((e, 2 * d), BF16), pltpu.VMEM((2, 2, 4, tok, d), BF16),
+                  pltpu.VMEM((mc, e), BF16), pltpu.VMEM((mc, e), BF16), pltpu.VMEM((mc, e), F32), pltpu.VMEM((mc, e), BF16))
+    gl_recv[me] = jnp.sum(gln_acc[...], axis=0, keepdims=True)
+    pass_on(0, 2)
+    gl = [rdma(gl_recv.at[me], gl_recv.at[me], gl_send.at[o - 1], gl_rsem.at[o - 1], lax.rem(me + o, 8)) for o in range(1, 8)]
+    for x in gl:
+        x.start()
+    finish(1, gwq_ref)
+    ag_forward()
+    for o in range(1, 8):
+        src = lax.rem(me + 8 - o, 8)
+        rdma(gl_recv.at[src], gl_recv.at[src], gl_send.at[o - 1], gl_rsem.at[o - 1], mate).wait_recv()
+    total = gl_recv[0]
+    for i in range(1, 8):
+        total = total + gl_recv[i]
+    gln_ref[...] = total
+    finish(0, gwo_ref)
+    ag_last()
+    for x in gl:
+        x.wait_send()
+    kp_copy.wait_send()
+    for dr in range(2):
+        for j in range(3):
+            hop_kv(dr, j).wait_send()
+            for s in range(2):
+                hop(s, dr, j).wait_send()
+
+
+def gradients(o, o_p, dq, dq_p, hn, hn_p, dy, dy_p, dkv, wqf, wof, w_kv, x, gain, cos_t, sin_t):
+    nb, tok, e = x.shape
+    n_tok = nb * tok
+    d = dq.shape[-1]
+    any_spec = pl.BlockSpec(memory_space=pl.ANY)
+    vmem = pl.BlockSpec(memory_space=pltpu.VMEM)
+    dma = pltpu.SemaphoreType.DMA
+    tokens = jax.ShapeDtypeStruct((n_tok, e), BF16)
+    y, gx, gln, gwo, gwq_t, gkv_t = pl.pallas_call(
+        functools.partial(grads_body, nb, tok),
+        in_specs=[any_spec] * 13 + [vmem, vmem, vmem],
+        out_specs=[any_spec, any_spec, vmem, vmem, vmem, any_spec],
+        out_shape=[tokens, tokens, jax.ShapeDtypeStruct((1, e), F32), jax.ShapeDtypeStruct((d, e), BF16),
+                   jax.ShapeDtypeStruct((d, e), BF16), jax.ShapeDtypeStruct((2, d, e), F32)],
+        scratch_shapes=[pltpu.VMEM((2, 4, 2, d, e // 2), F32), pltpu.VMEM((4, 2, d, e // 8), F32),
+                        pltpu.VMEM((2, 2, 3, d, e // 2), F32), pltpu.VMEM((2, 3, d, e // 8), F32),
+                        pltpu.VMEM((2, nb, tok, d), BF16), pltpu.VMEM((nb, tok, d), BF16), pltpu.VMEM((nb, tok, 2 * d), BF16),
+                        pltpu.VMEM((d, e // 4), F32), pltpu.VMEM((8, e), F32), pltpu.VMEM((8, 1, e), F32),
+                        dma((2, 2, 3)), dma((2, 2, 3)), dma((2, 3)), dma((2, 3)), dma((9,)), dma((9,)), dma((7,)), dma((7,)),
+                        dma((2,)), dma((2, 2)), dma((2,)), dma((6,))],
+        compiler_params=pltpu.CompilerParams(collective_id=2, has_side_effects=True, vmem_limit_bytes=63 * 2**20),
+        cost_estimate=pl.CostEstimate(flops=10 * n_tok * e * e, bytes_accessed=120 * 2**20, transcendentals=0),
+        name="gradients",
+    )(o, o_p, dq, dq_p, hn, hn_p, dy.reshape(n_tok, e), dy_p, dkv, wqf, wof.reshape(8 * d, e), w_kv, x.reshape(n_tok, e),
+      gain.reshape(1, e), cos_t, sin_t)
+    return y.reshape(nb, tok, e), gx.reshape(nb, tok, e), gln.reshape(e), gwq_t.T, gkv_t[0].T, gkv_t[1].T, gwo
 
 
 def solution(mesh):
@@ -534,29 +885,8 @@
         cos_t, sin_t = rope_tables(t0 + jnp.arange(tok), d)
 
         w_kv = jnp.concatenate([w_k, w_v], axis=1)
-        hn, q, do, kv_loc, wq_h, wo_h = project(x_loc, ln_scale, wq_loc, w_kv, wo_loc, dy_loc, cos_t, sin_t)
-        x_f32 = x_loc.astype(F32)
-        centered = x_f32 - jnp.mean(x_f32, axis=-1, keepdims=True)
-        inv_std = lax.rsqrt(jnp.mean(centered * centered, axis=-1, keepdims=True) + LN_EPS)
-        x_hat = centered * inv_std
-        ln_gain = ln_scale.astype(F32)
-
-        o, dq, dkv_loc = attention(q, do, kv_loc, cos_t, sin_t)
-        gwo = jnp.einsum('bhtd,bte->hde', o, dy_loc, preferred_element_type=F32)
-        gwo = lax.psum_scatter(gwo, 'tp', scatter_dimension=0, tiled=True)[0].astype(BF16)
-        gwq = jnp.einsum('bte,bhtd->hed', hn, dq, preferred_element_type=F32)
-        gwq = lax.psum_scatter(gwq, 'tp', scatter_dimension=0, tiled=True)[0].astype(BF16)
-        y = (x_f32 + jnp.einsum('bhtd,hde->bte', o, wo_h, preferred_element_type=F32)).astype(BF16)
-
-        dk_loc = rotate(dkv_loc[..., :d].astype(F32), cos_t, -sin_t).astype(BF16)
-        dkv_loc = jnp.concatenate([dk_loc, dkv_loc[..., d:]], axis=-1)
-        gwkv = jnp.einsum('bte,btd->ed', hn, dkv_loc, preferred_element_type=F32)
-        gwkv = lax.psum(gwkv, 'tp')
-        dhn = jnp.einsum('bhtd,hed->bte', dq, wq_h, preferred_element_type=F32)
-        dhn = dhn + jnp.einsum('btd,ed->bte', dkv_loc, w_kv, preferred_element_type=F32)
-        d_hat = dhn * ln_gain
-        grad_ln = lax.psum(jnp.sum(dhn * x_hat, axis=(0, 1)), 'tp')
-        grad_x = inv_std * (d_hat - jnp.mean(d_hat, axis=-1, keepdims=True) - x_hat * jnp.mean(d_hat * x_hat, axis=-1, keepdims=True)) + dy_loc.astype(F32)
-        return y, grad_x.astype(BF16), grad_ln, gwq, gwkv[:, :d], gwkv[:, d:], gwo
+        hn, q, do, kv_loc, wq_h, wo_h, hn_p, dy_p = project(x_loc, ln_scale, wq_loc, w_kv, wo_loc, dy_loc, cos_t, sin_t)
+        o, dq, dkv_loc, o_p, dq_p = attention(q, do, kv_loc, cos_t, sin_t)
+        return gradients(o, o_p, dq, dq_p, hn, hn_p, dy_loc, dy_p, dkv_loc, wq_h, wo_h, w_kv, x_loc, ln_scale, cos_t, sin_t)
 
     return jax.shard_map(device_step, mesh=mesh, in_specs=(act_spec, P(None), P(None, 'tp'), P(None, None), P(None, None), P('tp', None), act_spec), out_specs=(act_spec, act_spec, P('dp'), P('dp', 'tp'), P('dp', None), P('dp', None), P(('dp', 'tp'), None)), check_vma=False)

time: 521 us -> 476 us (0.914)
  Pallas kernels: 234 us -> 434 us
  waiting for transfers between devices: 107 us -> 0 us
  matrix products: 100 us -> 0 us
  other arithmetic: 28.9 us -> 0.43 us
  local copies, waits for them, and re-layouts: 13.4 us -> 32.4 us
  blocking collectives: 14.4 us -> 0 us
  between operations: 14.4 us -> 0.97 us
    pallas_call x0 -> x1, Pallas kernels: none -> 191 us  [gradients(): pl.pallas_call(functools.partial(grads_body, nb, tok), in_specs=[any_spec...]
    reduce_scatter x2 -> x0, waiting for transfers between devices: 107 us -> none  [the longest x1 86.6 us: device_step(): lax.psum_scatter(gwo, 'tp', scatter_dimension=0, tiled=True)[0].astype(BF16)]
    dot_general x6 -> x0, matrix products: 100 us -> none  [the longest x1 26.3 us: device_step(): dhn = jnp.einsum('bhtd,hed->bte', dq, wq_h, preferred_element_type=F32)]
    unnamed x16 -> x18, local copies, waits for them, and re-layouts: 4.55 us -> 24.5 us
    convert_element_type x5 -> x0, other arithmetic: 19.7 us -> none  [the longest x1 13.6 us: device_step(): return (y, grad_x.astype(BF16), grad_ln, gwq, gwkv[:, :d], gwkv[:, d:], gwo)]
    psum x1 -> x0, blocking collectives: 14.4 us -> none  [device_step(): grad_ln = lax.psum(jnp.sum(dhn * x_hat, axis=(0, 1)), 'tp')]
    pallas_call x1, Pallas kernels: 153 us -> 162 us  [attention(): pl.pallas_call(functools.partial(attn_body, nb, n_heads, tok, seq, d, gro...]
    reduce_sum x2 -> x0, other arithmetic: 8.54 us -> none  [the longest x1 4.7 us: device_step(): jnp.mean(centered * centered, axis=-1, keepdims=True) + LN_EPS]
  transfers between devices with their start and end apart: 3 -> 0, of which waited for: 2 -> 0; matrix products, arithmetic and copies ran while one was open for 24% -> 0% of each run, Pallas kernels for 0% -> 0%
where the time goes in v2:
time: 476 us; the launch traced here: 467 us
  Pallas kernels  434 us (91%)
  local copies, waits for them, and re-layouts  32.4 us (7%)
    pallas_call x1, Pallas kernels, gradients(): pl.pallas_call(functools.partial(grads_body, nb, tok), in_specs=[any_spec...  191 us
    pallas_call x1, Pallas kernels, attention(): pl.pallas_call(functools.partial(attn_body, nb, n_heads, tok, seq, d, gro...  162 us
    pallas_call x1, Pallas kernels, project(): pl.pallas_call(functools.partial(proj_body, nb, tok), in_specs=[any_spec,...  81 us
    unnamed x18, local copies, waits for them, and re-layouts  24.5 us

profile of v2, /device:TPU:112, one launch (start us, length us, event | category | flops | bytes accessed | tf_op | source)
XLA Modules:
  0.0 467.4 jit_solution(18314190125797216584)
XLA Ops:
  0.7 1.3 reshape.111.g_ref
  2.0 0.4 multiply_sine_fusion
  2.4 0.0 copy-start.2
  2.4 0.0 copy-start.3
  2.4 0.7 tile.20
  3.1 0.7 tile.8
  3.8 1.3 constant_dynamic-update-slice_fusion.1
  5.1 1.3 constant_dynamic-update-slice_fusion.wkv_ref.wkv_hbm
  6.4 0.0 copy-start.1
  6.4 1.3 copy-done.1
  7.8 81.0 %project.1 = (bf16[1536,2048]{1,0:T(8,128)(2,1)}, bf16[8,8,192,256]{3,2,1,0:T(8,128)(2,1)}, bf16[8,8,192,256]{3,2,1,0:T(8,128)(2,1)}, bf16[1536,512]{1,0:T(8,128...) custom-call(bf16[1536,2048]{1,0:T(8,128)(2,1)} %bitcast.24, ...), custom_call_target="tpu_custom_call" | custom-call | flops 28991029248 | bytes 62914560 | tf_op jit(solution)/shard_map/project/pallas_call | solution.py:527
  88.7 0.0 copy-done.2
  88.7 0.0 copy-done.3
  88.7 161.9 %attention.1 = (bf16[8,2,4,192,256]{4,3,2,1,0:T(8,128)(2,1)}, bf16[8,2,4,192,256]{4,3,2,1,0:T(8,128)(2,1)}, bf16[8,192,512]{2,1,0:T(8,128)(2,1)}, bf16[8,4,192,2...) custom-call(bf16[8,8,192,256]{3,2,1,0:T(8,128)(2,1)} %get-tuple-element.26.q_hbm, ...), custom_call_target="tpu_custom_call" | custom-call | flops 57982058496 | bytes 41943040 | tf_op jit(solution)/shard_map/attention/pallas_call | solution.py:343
  250.7 190.8 %gradients.1 = (bf16[1536,2048]{1,0:T(8,128)(2,1)}, bf16[1536,2048]{1,0:T(8,128)(2,1)}, f32[1,2048]{1,0:T(1,128)}, bf16[256,2048]{1,0:T(8,128)(2,1)}, bf16[256,2...) custom-call(bf16[8,2,4,192,256]{4,3,2,1,0:T(8,128)(2,1)} %get-tuple-element.29.o_hbm, ...), custom_call_target="tpu_custom_call" | custom-call | flops 64424509440 | bytes 125829120 | tf_op jit(solution)/shard_map/gradients/pallas_call | solution.py:858
  441.4 2.3 copy.14
  443.7 3.9 slice_bitcast_fusion
  447.6 2.9 copy.16
  450.5 1.8 copy.15
  452.3 6.6 %copy.22 = bf16[8,192,2048]{2,1,0:T(8,128)(2,1)} copy(bf16[8,192,2048]{2,1,0:T(8,128)(2,1)} %bitcast.19) | data formatting | bytes 12582912
  458.9 0.0 copy-start.4
  458.9 0.0 copy-start
  458.9 6.7 %copy.23 = bf16[8,192,2048]{2,1,0:T(8,128)(2,1)} copy(bf16[8,192,2048]{2,1,0:T(8,128)(2,1)} %bitcast.18) | data formatting | bytes 12582912
  465.6 0.0 copy-done.4
  465.6 0.6 copy.24
  466.2 0.0 copy-done
  466.2 1.0 copy.25
  (2 shorter events, 0.0 us)
Async XLA Ops:
  2.4 86.3 %copy-start.2 = (f32[192,128]{1,0:T(8,128)}, f32[192,128]{1,0:T(8,128)S(1)}, u32[]{:S(2)}) copy-start(f32[192,128]{1,0:T(8,128)S(1)} %get-tuple-element.54.sin_ref) | copy-start | bytes 294916
  2.4 86.3 %copy-start.3 = (f32[192,128]{1,0:T(8,128)}, f32[192,128]{1,0:T(8,128)S(1)}, u32[]{:S(2)}) copy-start(f32[192,128]{1,0:T(8,128)S(1)} %get-tuple-element.55.cos_ref) | copy-start | bytes 294916
  6.4 1.3 copy-start.1
  458.9 6.7 %copy-start.4 = (f32[1,2048]{1,0:T(1,128)S(1)}, f32[1,2048]{1,0:T(1,128)}, u32[]{:S(2)}) copy-start(f32[1,2048]{1,0:T(1,128)} %get-tuple-element.41) | copy-start | bytes 24580
  458.9 7.3 %copy-start = (bf16[256,2048]{1,0:T(8,128)(2,1)S(1)}, bf16[256,2048]{1,0:T(8,128)(2,1)}, u32[]{:S(2)}) copy-start(bf16[256,2048]{1,0:T(8,128)(2,1)} %get-tuple-element.69) | copy-start | bytes 3145732

commit v3 on v2

--- a/solution.py
+++ b/solution.py
@@ -53,13 +53,15 @@
     pl.semaphore_wait(barrier, len(peers))
 
 
-def attn_body(nb, n_heads, tok, seq, d, group, q_hbm, do_hbm, kvl_hbm, cos_ref, sin_ref,
+def attn_body(nb, tok, seq, d, q_hbm, do_hbm, kvl_hbm, cos_ref, sin_ref,
               o_hbm, dq_hbm, dkv_hbm, op_hbm, dqp_hbm,
-              kv_all, q_v, do_v, o_v, dq_v, bias, s_buf, p_buf, ds_buf, mrecv, rrecv,
+              kv_all, q_v, do_v, o_v, dq_v, s_buf, m_buf, l_buf, p_buf, ds_buf, q_t, do_t, dk_t, dv_t, d_buf, cos4, sin4, mrecv, rrecv,
               kv_send, kv_recv, m_send, m_recv, r_send, r_recv, own_sem, in_sem, out_sem, fin_sem, p_send, p_recv):
     scale = d ** -0.5
-    rows = group * tok
-    kb = 256
+    rows = s_buf.shape[1]
+    n_blk = seq // 256
+    rb = 2 * rows // n_blk
+    n_rb = rows // rb
     half = d // 2
     me, k, mate, cw, ccw = ring_ids()
     c = me // 2
@@ -193,13 +195,97 @@
         return (pltpu.make_async_copy(q_hbm.at[b], q_v.at[slot], in_sem.at[0, slot]),
                 pltpu.make_async_copy(do_hbm.at[b], do_v.at[slot], in_sem.at[1, slot]))
 
-    def store(b, slot):
-        return (pltpu.make_async_copy(o_v.at[slot], o_hbm.at[b], out_sem.at[0, slot]),
-                pltpu.make_async_copy(dq_v.at[slot], dq_hbm.at[b], out_sem.at[1, slot]))
-
-    def hand(b, slot):
-        return (rdma(o_v.at[slot, 1 - k], op_hbm.at[b], p_send.at[0, b], p_recv.at[0, b], mate),
-                rdma(dq_v.at[slot, 1 - k], dqp_hbm.at[b], p_send.at[1, b], p_recv.at[1, b], mate))
+    def handed(dst, src, n, b, slot):
+        return rdma(src.at[slot, 1 - k], dst.at[b], p_send.at[n, b], p_recv.at[n, b], mate)
+
+    def store_o(b, slot):
+        return (pltpu.make_async_copy(o_v.at[slot], o_hbm.at[b], out_sem.at[0, slot]), handed(op_hbm, o_v, 0, b, slot))
+
+    def store_dq(b, slot):
+        return (pltpu.make_async_copy(dq_v.at[slot], dq_hbm.at[b], out_sem.at[1, slot]), handed(dqp_hbm, dq_v, 1, b, slot))
+
+    def stored(x):
+        x[0].wait()
+        x[1].wait_send()
+
+    def scores(b, g, slot, i):
+        cols = slice(i * 256, (i + 1) * 256)
+        s = dot_nt(q_v[slot, g].reshape(rows, d), kv_all[b, cols, :d])
+        col = lax.broadcasted_iota(jnp.int32, (tok, 256), 1) + i * 256
+        row = lax.broadcasted_iota(jnp.int32, (tok, 256), 0) + me * tok
+        s = jnp.concatenate([jnp.where(col <= row, s[j * tok:(j + 1) * tok], -1e30) for j in range(rows // tok)], axis=0)
+        s_buf[g, :, cols] = s
+        m = jnp.maximum(s[:, :128], s[:, 128:])
+        m_buf[...] = m if i == 0 else jnp.maximum(m_buf[...], m)
+
+    def softmax(g, i):
+        n = rows // n_blk
+        for r in range(i * n, (i + 1) * n, 16):
+            rs = slice(r, r + 16)
+            m = jnp.max(m_buf[rs, :], axis=1, keepdims=True) * (scale * LOG2E)
+            l = None
+            for j in range(0, seq, 128):
+                e = jnp.exp2(s_buf[g, rs, j:j + 128] * (scale * LOG2E) - m)
+                s_buf[g, rs, j:j + 128] = e
+                l = e if l is None else l + e
+            l_buf[g, rs, :] = jnp.broadcast_to(1.0 / jnp.sum(l, axis=1, keepdims=True), (16, 128))
+
+    def turn(g, slot, i):
+        rs = slice(i * rb, (i + 1) * rb)
+        q_t[g, :, rs] = q_v[slot, g].reshape(rows, d)[rs].T
+        do_t[g, :, rs] = do_v[slot, g].reshape(rows, d)[rs].T
+
+    def out_rows(b, g, slot, i):
+        rs = slice(i * rb, (i + 1) * rb)
+        p = (s_buf[g, rs, :] * jnp.concatenate([l_buf[g, rs, :]] * (seq // 128), axis=1)).astype(BF16)
+        p_buf[rs, :] = p
+        o = dot_nn(p, kv_all[b, :, d:])
+        dvec = jnp.sum(o * do_v[slot, g].reshape(rows, d)[rs].astype(F32), axis=1, keepdims=True)
+        d_buf[rs, :] = jnp.broadcast_to(dvec, (rb, 128))
+        put_rows(o_v, slot, g, i, o.astype(BF16))
+
+    def put_rows(ref, slot, g, i, v):
+        r = i * rb
+        while r < (i + 1) * rb:
+            n = min((i + 1) * rb - r, tok - r % tok)
+            ref[slot, g, r // tok, r % tok:r % tok + n, :] = v[r - i * rb:r - i * rb + n]
+            r += n
+
+    def dq_rows(b, g, slot, i):
+        rs = slice(i * rb, (i + 1) * rb)
+        dq = dot_nn(ds_buf[rs, :], kv_all[b, :, :d]) * scale
+        lo, hi = dq[:, :half], dq[:, half:]
+        cs, sn = cos4[rs, :], sin4[rs, :]
+        put_rows(dq_v, slot, g, i, jnp.concatenate([(lo * cs + hi * sn).astype(BF16), (hi * cs - lo * sn).astype(BF16)], axis=1))
+
+    def grads(b, g, slot, i):
+        cols = slice(i * 256, (i + 1) * 256)
+        do = do_v[slot, g].reshape(rows, d)
+        p = p_buf[:, cols]
+        dp = dot_nt(do, kv_all[b, cols, d:])
+        dvec = d_buf[...]
+        if i > 0:
+            n = rows // n_blk
+            z = l_buf[1 - g, (i - 1) * n:(i - 1) * n + 8, :]
+            for r in range(8, n, 8):
+                z = jnp.minimum(z, l_buf[1 - g, (i - 1) * n + r:(i - 1) * n + r + 8, :])
+            dvec = dvec + jnp.concatenate([jnp.minimum(z, 0.0)] * (rows // 8), axis=0)
+        dd = jnp.concatenate([dvec, dvec], axis=1)
+        ds = (p.astype(F32) * (dp - dd)).astype(BF16)
+        ds_buf[:, cols] = ds
+        dk = dot_nn(q_t[g], ds)
+        dv = dot_nn(do_t[g], p)
+        if g == 0:
+            dk_t[:, cols] = dk
+            dv_t[:, cols] = dv
+        else:
+            dk_t[:, cols] += dk
+            dv_t[:, cols] += dv
+
+    def close_kv(b, i):
+        cols = slice(i * 256, (i + 1) * 256)
+        kv_all[b, cols, :d] = (dk_t[:, cols] * scale).T.astype(BF16)
+        kv_all[b, cols, d:] = dv_t[:, cols].T.astype(BF16)
 
     enter((mate, cw, ccw))
     for b in range(nb):
@@ -213,17 +299,34 @@
     def _(j):
         for b in range(nb):
             kv_all[b, blk(j), :] = jnp.zeros((tok, 2 * d), BF16)
-    t0 = me * tok
-    row = lax.broadcasted_iota(jnp.int32, (tok, seq), 0) + t0
-    col = lax.broadcasted_iota(jnp.int32, (tok, seq), 1)
-    bias[...] = jnp.where(col <= row, F32(3.0e38), F32(-1e30))
+    for j in range(rows // tok):
+        cos4[j * tok:(j + 1) * tok, :] = cos_ref[...]
+        sin4[j * tok:(j + 1) * tok, :] = sin_ref[...]
+    ds_buf[...] = jnp.zeros_like(ds_buf)
     for b in range(min(2, nb)):
         service_a(b)
     service_b(0)
+    for x in load(0, 0):
+        x.wait()
+    for i in range(n_rb):
+        turn(0, 0, i)
+    ready(0)
+    for i in range(n_blk):
+        scores(0, 0, 0, i)
+    for i in range(n_blk):
+        softmax(0, i)
+
+    def comm_steps(b):
+        for lag, stage in ((2, stage1), (3, stage2), (4, stage3)):
+            @pl.when((b >= lag) & (b - lag < nb))
+            def _():
+                stage(b - lag)
 
     @pl.loop(0, nb)
     def _(b):
         slot = lax.rem(b, 2)
+        nxt = jnp.minimum(b + 1, nb - 1)
+        prev = jnp.maximum(b - 1, 0)
 
         @pl.when(b + 1 < nb)
         def _():
@@ -241,86 +344,75 @@
         @pl.when(b + 1 < nb)
         def _():
             service_b(b + 1)
+        comm_steps(b)
 
         @pl.when(b >= 1)
         def _():
-            stage1(b - 1)
+            drain_kv(b - 1)
 
         @pl.when(b >= 2)
         def _():
-            stage2(b - 2)
-            for x in store(b - 2, slot):
+            stored(store_o(b - 2, slot))
+        spare = jnp.where(b >= 1, b - 1, nb)
+        for i in range(n_blk):
+            scores(b, 1, slot, i)
+            if i % 2 == 1:
+                out_rows(b, 0, slot, i // 2)
+                dq_rows(prev, 1, 1 - slot, i // 2)
+                turn(1, slot, i // 2)
+        for i in range(n_blk):
+            close_kv(spare, i)
+
+        @pl.when(b >= 1)
+        def _():
+            for x in store_dq(b - 1, 1 - slot):
+                x.start()
+            to_mate(b - 1)
+        for i in range(n_blk):
+            grads(b, 0, slot, i)
+            softmax(1, i)
+
+        @pl.when(b + 1 < nb)
+        def _():
+            for x in load(b + 1, 1 - slot):
                 x.wait()
-            for x in hand(b - 2, slot):
-                x.wait_send()
-
-        @pl.when(b >= 3)
-        def _():
-            stage3(b - 3)
-        for x in load(b, slot):
-            x.wait()
-        ready(b)
-        k_ref = kv_all.at[b, :, :d]
-        v_ref = kv_all.at[b, :, d:]
-        dk_acc = dv_acc = None
-        for g in range(n_heads // group):
-            q = jnp.concatenate([q_v[slot, g * group + j] for j in range(group)], axis=0)
-            do = jnp.concatenate([do_v[slot, g * group + j] for j in range(group)], axis=0)
-            for i in range(seq // kb):
-                cols = slice(i * kb, (i + 1) * kb)
-                s_buf[:, cols] = dot_nt(q, k_ref[cols, :])
-            rb = 16
-            for r in range(rows // rb):
-                rs = slice(r * rb, (r + 1) * rb)
-                t = (r * rb) % tok
-                s = jnp.minimum(s_buf[rs, :], bias[t:t + rb, :])
-                m = jnp.max(s, axis=1, keepdims=True)
-                e = jnp.exp2(s * (scale * LOG2E) - m * (scale * LOG2E))
-                l = jnp.sum(e, axis=1, keepdims=True)
-                p_buf[rs, :] = (e * (1.0 / l)).astype(BF16)
-            o = dot_nn(p_buf[...], v_ref[...])
-            dvec = jnp.sum(o * do.astype(F32), axis=1, keepdims=True)
-            o16 = o.astype(BF16)
-            for j in range(group):
-                o_v[slot, j % 2, (g * group + j) // 2] = o16[j * tok:(j + 1) * tok]
-            dv_t = dot_nn(do.T, p_buf[...])
-            for i in range(seq // kb):
-                cols = slice(i * kb, (i + 1) * kb)
-                dp = dot_nt(do, v_ref[cols, :])
-                ds_buf[:, cols] = (p_buf[:, cols].astype(F32) * (dp - dvec)).astype(BF16)
-            dq = dot_nn(ds_buf[...], k_ref[...]) * scale
-            dk_t = dot_nn(q.T, ds_buf[...])
-            for j in range(group):
-                part = dq[j * tok:(j + 1) * tok]
-                lo, hi = part[:, :half], part[:, half:]
-                cs, sn = cos_ref[...], sin_ref[...]
-                dq_v[slot, j % 2, (g * group + j) // 2, :, :half] = (lo * cs + hi * sn).astype(BF16)
-                dq_v[slot, j % 2, (g * group + j) // 2, :, half:] = (hi * cs - lo * sn).astype(BF16)
-            dk_acc = dk_t if g == 0 else dk_acc + dk_t
-            dv_acc = dv_t if g == 0 else dv_acc + dv_t
-        drain_kv(b)
-        kv_all[b, :, :d] = (dk_acc * scale).T.astype(BF16)
-        kv_all[b, :, d:] = dv_acc.T.astype(BF16)
-        for x in store(b, slot) + hand(b, slot):
+            ready(b + 1)
+
+        @pl.when(b >= 2)
+        def _():
+            stored(store_dq(b - 2, slot))
+        nslot = lax.rem(nxt, 2)
+        for i in range(n_blk):
+            scores(nxt, 0, nslot, i)
+            if i % 2 == 1:
+                out_rows(b, 1, slot, i // 2)
+                dq_rows(b, 0, slot, i // 2)
+                turn(0, nslot, i // 2)
+        for x in store_o(b, slot):
             x.start()
-        to_mate(b)
+        for i in range(n_blk):
+            grads(b, 1, slot, i)
+            softmax(0, i)
 
     n = nb
-    stage1(n - 1)
-    stage2(n - 2)
-    if n >= 3:
-        stage3(n - 3)
-    stage2(n - 1)
-    stage3(n - 2)
-    stage3(n - 1)
+    drain_kv(n - 1)
+    for i in range(n_rb):
+        dq_rows(n - 1, 1, (n - 1) % 2, i)
+    for i in range(n_blk):
+        close_kv(n - 1, i)
+    for x in store_dq(n - 1, (n - 1) % 2):
+        x.start()
+    to_mate(n - 1)
+    for b in range(n, n + 4):
+        for lag, stage in ((2, stage1), (3, stage2), (4, stage3)):
+            if 0 <= b - lag < n:
+                stage(b - lag)
     for b in (n - 2, n - 1):
-        for x in store(b, b % 2):
-            x.wait()
-        for x in hand(b, b % 2):
-            x.wait_send()
+        stored(store_o(b, b % 2))
+        stored(store_dq(b, b % 2))
     for b in range(n):
-        for x in hand(b, b % 2):
-            x.wait_recv()
+        handed(op_hbm, o_v, 0, b, b % 2).wait_recv()
+        handed(dqp_hbm, dq_v, 1, b, b % 2).wait_recv()
         fin_copy(b).wait()
         for cond, slot in ((c == 3, 0), (c >= 1, 1), (c >= 2, 2)):
             @pl.when(cond)
@@ -329,31 +421,32 @@
 
 
 def attention(q, do, kv, cos_t, sin_t):
-    nb, n_heads, tok, d = q.shape
+    nb, _, hp, tok, d = q.shape
     seq = tok * 8
-    group = 4
-    rows = group * tok
+    rows = hp * tok
     any_spec = pl.BlockSpec(memory_space=pl.ANY)
     vmem = pl.BlockSpec(memory_space=pltpu.VMEM)
     dma = pltpu.SemaphoreType.DMA
-    slab = pltpu.VMEM((2, n_heads, tok, d), BF16)
-    oslab = pltpu.VMEM((2, 2, n_heads // 2, tok, d), BF16)
-    out = jax.ShapeDtypeStruct((nb, 2, n_heads // 2, tok, d), BF16)
-    outp = jax.ShapeDtypeStruct((nb, n_heads // 2, tok, d), BF16)
+    slab = pltpu.VMEM((2, 2, hp, tok, d), BF16)
+    out = jax.ShapeDtypeStruct(q.shape, BF16)
+    outp = jax.ShapeDtypeStruct((nb, hp, tok, d), BF16)
     return pl.pallas_call(
-        functools.partial(attn_body, nb, n_heads, tok, seq, d, group),
+        functools.partial(attn_body, nb, tok, seq, d),
         in_specs=[any_spec, any_spec, any_spec, vmem, vmem],
         out_specs=[any_spec] * 5,
         out_shape=[out, out, jax.ShapeDtypeStruct(kv.shape, BF16), outp, outp],
-        scratch_shapes=[pltpu.VMEM((nb, seq, 2 * d), BF16), slab, slab, oslab, oslab,
-                        pltpu.VMEM((tok, seq), F32), pltpu.VMEM((rows, seq), F32),
-                        pltpu.VMEM((rows, seq), BF16), pltpu.VMEM((rows, seq), BF16),
+        scratch_shapes=[pltpu.VMEM((nb + 1, seq, 2 * d), BF16), slab, slab, slab, slab,
+                        pltpu.VMEM((2, rows, seq), F32), pltpu.VMEM((rows, 128), F32),
+                        pltpu.VMEM((2, rows, 128), F32), pltpu.VMEM((rows, seq), BF16), pltpu.VMEM((rows, seq), BF16),
+                        pltpu.VMEM((2, d, rows), BF16), pltpu.VMEM((2, d, rows), BF16),
+                        pltpu.VMEM((d, seq), F32), pltpu.VMEM((d, seq), F32), pltpu.VMEM((rows, 128), F32),
+                        pltpu.VMEM((rows, d // 2), F32), pltpu.VMEM((rows, d // 2), F32),
                         pltpu.VMEM((nb, 4, tok, 2 * d), BF16), pltpu.VMEM((nb, 3, tok, 2 * d), BF16),
                         dma((nb, 7)), dma((nb, 7)), dma((nb, 4)), dma((nb, 4)), dma((nb, 3)), dma((nb, 3)),
                         dma((nb,)), dma((2, 2)), dma((2, 2)), dma((nb,)), dma((2, nb)), dma((2, nb))],
         compiler_params=pltpu.CompilerParams(collective_id=1, has_side_effects=True, vmem_limit_bytes=63 * 2**20),
-        cost_estimate=pl.CostEstimate(flops=12 * nb * n_heads * tok * seq * d, bytes_accessed=40 * 2**20,
-                                      transcendentals=nb * n_heads * tok * seq),
+        cost_estimate=pl.CostEstimate(flops=24 * nb * rows * seq * d, bytes_accessed=40 * 2**20,
+                                      transcendentals=2 * nb * rows * seq),
         name="attention",
     )(q, do, kv, cos_t, sin_t)
 
@@ -470,7 +563,7 @@
                 out_v[slot, pl.ds(2 * i, 2), :, half:] = o1
             else:
                 out_v[slot, pl.ds(2 * i, 2)] = dot_nt(dy_v[rs, :], wo_v[h]).reshape(2, tok, d).astype(BF16)
-        c = pltpu.make_async_copy(out_v.at[slot], (q_hbm, do_hbm)[w].at[:, h], out_sem.at[slot])
+        c = pltpu.make_async_copy(out_v.at[slot], (q_hbm, do_hbm)[w].at[:, lax.rem(h, 2), h // 2], out_sem.at[slot])
         c.start()
         outs.append(c)
         save(w, h)
@@ -520,7 +613,7 @@
     n_tok = nb * tok
     any_spec = pl.BlockSpec(memory_space=pl.ANY)
     vmem = pl.BlockSpec(memory_space=pltpu.VMEM)
-    act = jax.ShapeDtypeStruct((nb, n_heads, tok, d), BF16)
+    act = jax.ShapeDtypeStruct((nb, 2, n_heads // 2, tok, d), BF16)
     dma = pltpu.SemaphoreType.DMA
     flops = 2 * n_tok * e * (2 * n_heads + 2) * d
     cos2, sin2 = jnp.tile(cos_t, (2, 1)), jnp.tile(sin_t, (2, 1))

time: 476 us -> 450 us (0.945)
  the two profiles are of different devices: /device:TPU:112 before, /device:TPU:113 now
where the time goes in v3:
time: 450 us; the launch traced here: 441 us
  Pallas kernels  407 us (90%)
  local copies, waits for them, and re-layouts  32.4 us (7%)
    pallas_call x1, Pallas kernels, gradients(): pl.pallas_call(functools.partial(grads_body, nb, tok), in_specs=[any_spec...  194 us
    pallas_call x1, Pallas kernels, attention(): pl.pallas_call(functools.partial(attn_body, nb, tok, seq, d), in_specs=[a...  132 us
    pallas_call x1, Pallas kernels, project(): pl.pallas_call(functools.partial(proj_body, nb, tok), in_specs=[any_spec,...  81.4 us
    unnamed x18, local copies, waits for them, and re-layouts  24.5 us

profile of v3, /device:TPU:113, one launch (start us, length us, event | category | flops | bytes accessed | tf_op | source)
XLA Modules:
  0.0 441.2 jit_solution(12926498557965830437)
XLA Ops:
  0.7 1.3 reshape.111.g_ref
  2.0 0.4 multiply_sine_fusion
  2.4 0.0 copy-start.2
  2.4 0.0 copy-start.3
  2.4 0.7 tile.20
  3.1 0.7 tile.8
  3.8 1.3 constant_dynamic-update-slice_fusion.1
  5.1 1.3 constant_dynamic-update-slice_fusion.wkv_ref.wkv_hbm
  6.4 0.0 copy-start.1
  6.4 1.3 copy-done.1
  7.8 81.4 %project.1 = (bf16[1536,2048]{1,0:T(8,128)(2,1)}, bf16[8,2,4,192,256]{4,3,2,1,0:T(8,128)(2,1)}, bf16[8,2,4,192,256]{4,3,2,1,0:T(8,128)(2,1)}, bf16[1536,512]{1,0...) custom-call(bf16[1536,2048]{1,0:T(8,128)(2,1)} %bitcast.24, ...), custom_call_target="tpu_custom_call" | custom-call | flops 28991029248 | bytes 62914560 | tf_op jit(solution)/shard_map/project/pallas_call | solution.py:620
  89.2 0.0 copy-done.2
  89.2 0.0 copy-done.3
  89.2 132.0 %attention.1 = (bf16[8,2,4,192,256]{4,3,2,1,0:T(8,128)(2,1)}, bf16[8,2,4,192,256]{4,3,2,1,0:T(8,128)(2,1)}, bf16[8,192,512]{2,1,0:T(8,128)(2,1)}, bf16[8,4,192,2...) custom-call(bf16[8,2,4,192,256]{4,3,2,1,0:T(8,128)(2,1)} %get-tuple-element.26.q_hbm, ...), custom_call_target="tpu_custom_call" | custom-call | flops 57982058496 | bytes 41943040 | tf_op jit(solution)/shard_map/attention/pallas_call | solution.py:433
  221.2 193.9 %gradients.1 = (bf16[1536,2048]{1,0:T(8,128)(2,1)}, bf16[1536,2048]{1,0:T(8,128)(2,1)}, f32[1,2048]{1,0:T(1,128)}, bf16[256,2048]{1,0:T(8,128)(2,1)}, bf16[256,2...) custom-call(bf16[8,2,4,192,256]{4,3,2,1,0:T(8,128)(2,1)} %get-tuple-element.29.o_hbm, ...), custom_call_target="tpu_custom_call" | custom-call | flops 64424509440 | bytes 125829120 | tf_op jit(solution)/shard_map/gradients/pallas_call | solution.py:951
  415.0 2.3 copy.14
  417.3 3.9 slice_bitcast_fusion
  421.2 2.9 copy.16
  424.1 1.8 copy.15
  425.9 6.6 %copy.22 = bf16[8,192,2048]{2,1,0:T(8,128)(2,1)} copy(bf16[8,192,2048]{2,1,0:T(8,128)(2,1)} %bitcast.19) | data formatting | bytes 12582912
  432.5 0.0 copy-start.4
  432.5 0.0 copy-start
  432.5 6.7 %copy.23 = bf16[8,192,2048]{2,1,0:T(8,128)(2,1)} copy(bf16[8,192,2048]{2,1,0:T(8,128)(2,1)} %bitcast.18) | data formatting | bytes 12582912
  439.2 0.0 copy-done.4
  439.2 0.6 copy.24
  439.8 0.0 copy-done
  439.8 1.0 copy.25
  (2 shorter events, 0.0 us)
Async XLA Ops:
  2.4 86.8 %copy-start.2 = (f32[192,128]{1,0:T(8,128)}, f32[192,128]{1,0:T(8,128)S(1)}, u32[]{:S(2)}) copy-start(f32[192,128]{1,0:T(8,128)S(1)} %get-tuple-element.54.sin_ref) | copy-start | bytes 294916
  2.4 86.8 %copy-start.3 = (f32[192,128]{1,0:T(8,128)}, f32[192,128]{1,0:T(8,128)S(1)}, u32[]{:S(2)}) copy-start(f32[192,128]{1,0:T(8,128)S(1)} %get-tuple-element.55.cos_ref) | copy-start | bytes 294916
  6.4 1.3 copy-start.1
  432.5 6.7 %copy-start.4 = (f32[1,2048]{1,0:T(1,128)S(1)}, f32[1,2048]{1,0:T(1,128)}, u32[]{:S(2)}) copy-start(f32[1,2048]{1,0:T(1,128)} %get-tuple-element.41) | copy-start | bytes 24580
  432.5 7.3 %copy-start = (bf16[256,2048]{1,0:T(8,128)(2,1)S(1)}, bf16[256,2048]{1,0:T(8,128)(2,1)}, u32[]{:S(2)}) copy-start(bf16[256,2048]{1,0:T(8,128)(2,1)} %get-tuple-element.69) | copy-start | bytes 3145732
